TPU v7x, 128 devices: a whole 4x4x4 slice. The times are simulated.
128 devices in a mesh: probe: 32 (over y, z_hi, x), tile: 4 (over z_lo, core).
Axes of the slice: x: 4, y: 4, z: 4 (z_hi: 2, z_lo: 2; z = z_hi * 2 + z_lo), core: 2. Of those that a mesh axis runs over, the one named last changes fastest.
Arguments:
- transmission: bfloat16 [2, 2, 2048, 1024], P(None, None, 'tile', 'probe'), may hold values from -4.1875 to 4.1875
- illumination: bfloat16 [2, 512, 512], replicated, may hold values from -3 to 3
- intensities: float32 [64, 512, 512], P('probe'), may hold values from 0 to 1
- scan_positions: int32 [64, 2], P('probe'), may hold values from 0 to 512, as said below
- tile_owner: int32 [64], P('probe'), may hold values from 0 to 3, as said below
Outputs:
- gradient: float32 [2, 2, 2048, 1024], P(None, None, 'tile', 'probe')
- probe_losses: float32 [64], P('probe')
Inputs may be any that keep to these rules, and one draw needn't show every extreme that they name: `tile_owner`: of the 2 scan positions held by one device along probe, no two have the same owner. scan_positions[k, 0] counts rows from row tile_owner[k] * 512 - 128 of the object and scan_positions[k, 1] columns from its first column; the 512 x 512 window of every probe lies inside the object and inside its owner's rows widened by 128 on each side.
All inputs are finite; a program needn't handle non-finite values.
Results may differ from a plain program's by a relative error of at most 0.012.
Values may be sent and summed in bfloat16 or wider, within the bound.
No kernel may reach another device: no remote copies, remote signals or barrier semaphores. Data moves between devices by JAX's collectives and lax.ppermute only.
A program may use at most 128 MiB of HBM per device.

v0:
```python
import math

import jax
import jax.numpy as jnp
import numpy as np
from jax import lax
from jax.sharding import PartitionSpec as P

FRAME = 512
BORDER = 128
TILE_ROWS = 512
FRESNEL = 0.25
ALL = ("probe", "tile")
BF = jnp.bfloat16
F32 = jnp.float32


def natural(order):
    return order // 256 * 256 + order % 8 * 32 + order // 8 % 32


def build_tables():
    n = FRAME
    index = np.arange(n)
    angle = (np.float32(-2.0 * math.pi) * (np.outer(index, index) % n).astype(np.float32) / np.float32(n)).astype(np.float32)
    norm = np.float32(1.0 / math.sqrt(n))
    wave_re, wave_im = np.cos(angle) * norm, np.sin(angle) * norm
    freq = np.where(index < n // 2, index, index - n).astype(np.float32)
    phase = (np.float32(-math.pi * FRESNEL) * freq * freq / np.float32(n)).astype(np.float32)
    kre, kim = np.cos(phase)[:, None], np.sin(phase)[:, None]
    sre, sim = kre * wave_re - kim * wave_im, kre * wave_im + kim * wave_re
    prop_re = wave_re @ sre + wave_im @ sim
    prop_im = wave_re @ sim - wave_im @ sre
    perm = natural(index)
    bf = jnp.bfloat16
    far = (wave_re[perm].astype(bf), wave_im[perm].astype(bf))
    prop = (prop_re[perm][:, perm].astype(bf), prop_im[perm][:, perm].astype(bf))
    return far, prop


def dot(left, right, dims):
    return lax.dot_general(left, right, (dims, ((), ())), preferred_element_type=F32)


def cdot(left, right, dims, conj_left=False, conj_right=False):
    lre, lim = left
    rre, rim = right
    ii = dot(lim, rim, dims)
    rr = dot(lre, rre, dims)
    ri = dot(lre, rim, dims)
    ir = dot(lim, rre, dims)
    re = rr + ii if conj_left != conj_right else rr - ii
    if conj_left:
        ir = -ir
    if conj_right:
        ri = -ri
    return re, ri + ir


def rounded(pair):
    return tuple(v.astype(BF) for v in pair)


NN = ((1,), (0,))
TN = ((0,), (0,))
NT = ((1,), (1,))


def body(transmission, illumination, intensities, scan_positions, tile_owner):
    far_np, prop_np = build_tables()
    far = tuple(jnp.asarray(v) for v in far_np)
    prop = tuple(jnp.asarray(v) for v in prop_np)
    device = lax.axis_index("probe") * 4 + lax.axis_index("tile")
    core = lax.axis_index("tile") % 2
    which = lax.axis_index("tile") // 2
    my_col = device // 4
    my_quarter = device % 4
    order = jnp.arange(FRAME, dtype=jnp.int32)
    residue = natural(order)

    row0 = tile_owner * TILE_ROWS - BORDER + scan_positions[:, 0]
    col0 = scan_positions[:, 1]
    info = jnp.stack([row0 // 32, row0 % 32, col0 // 32, col0 % 32], axis=1).reshape(8).astype(BF)
    place = (residue[None, :] == order[:, None]).astype(BF)
    block = dot(transmission.reshape(4, 512, 32), place, ((1,), (0,))).astype(BF)
    block = block.reshape(4, 32, 4, 128).transpose(1, 2, 0, 3).reshape(128, 4, 128)
    info = jnp.broadcast_to(jnp.pad(info, (0, 120)), (128, 4, 128))
    got = lax.all_to_all(jnp.concatenate([block, info], axis=1), ALL, 0, 0, tiled=True)
    told = got[::4, 4, :8].astype(jnp.int32).reshape(64, 4)
    rows0 = told[:, 0] * 32 + told[:, 1]
    cols0 = told[:, 2] * 32 + told[:, 3]

    cand = got[:, :4].reshape(2, 16, 4, 4, 128).transpose(0, 2, 3, 1, 4)
    column = jnp.arange(16, dtype=jnp.int32) * 32 + my_col
    row = natural(my_quarter * 128 + jnp.arange(128, dtype=jnp.int32))
    half = (column[None, :] < cols0[:, None]).astype(jnp.int32)
    tile = rows0[:, None] // 512 + (row[None, :] < rows0[:, None] % 512)
    pick = tile[:, None, :] + 4 * half[:, :, None]
    sent = jnp.zeros((64, 4, 16, 128), BF)
    for a in range(2):
        for b in range(4):
            sent = jnp.where((pick == 4 * a + b)[:, None], cand[a, b][None], sent)
    sent = sent.reshape(64, 4, 2, 8, 128).transpose(0, 2, 1, 3, 4).reshape(128, 32, 128)
    mine = lax.all_to_all(sent, ALL, 0, 0, tiled=True)
    mine = mine.reshape(32, 4, 4, 8, 128).transpose(2, 0, 3, 1, 4).reshape(4, 256, 512)
    swap = [(0, 1), (1, 0), (2, 3), (3, 2)]
    other = lax.ppermute(mine, "tile", swap)
    first = core == 0
    patch = jnp.concatenate([jnp.where(first, mine, other), jnp.where(first, other, mine)], axis=1)

    my_row0 = lax.dynamic_index_in_dim(row0, which, 0, False)
    my_col0 = lax.dynamic_index_in_dim(col0, which, 0, False)
    roll_cols = ((residue[:, None] - my_col0) % FRAME == order[None, :]).astype(BF)
    roll_rows = ((residue[None, :] - my_row0) % FRAME == order[:, None]).astype(BF)
    wave = []
    for v in (illumination[0], illumination[1]):
        turned = dot(roll_cols, v, NT).astype(BF)
        wave.append(dot(turned, roll_rows, NN))
    layer = patch.astype(F32)
    exit0 = (wave[0] * layer[0] - wave[1] * layer[1], wave[0] * layer[1] + wave[1] * layer[0])
    inner = rounded(cdot(rounded(exit0), prop, NN))
    mid = cdot(prop, inner, NN)
    exit1 = (mid[0] * layer[2] - mid[1] * layer[3], mid[0] * layer[3] + mid[1] * layer[2])
    inner = rounded(cdot(rounded(exit1), far, NN))
    psi = cdot(inner, far, TN)
    measured = lax.dynamic_index_in_dim(intensities, which, 0, False)
    misfit = psi[0] * psi[0] + psi[1] * psi[1] - measured
    loss = jnp.mean(misfit * misfit)
    inner = rounded(cdot(far, rounded((misfit * psi[0], misfit * psi[1])), NT, conj_left=True))
    back = cdot(inner, far, NT, conj_right=True)
    grad1 = (mid[0] * back[0] + mid[1] * back[1], mid[0] * back[1] - mid[1] * back[0])
    carry = (layer[2] * back[0] + layer[3] * back[1], layer[2] * back[1] - layer[3] * back[0])
    inner = rounded(cdot(rounded(carry), prop, NN, conj_right=True))
    back = cdot(prop, inner, NN, conj_left=True)
    grad0 = (wave[0] * back[0] + wave[1] * back[1], wave[0] * back[1] - wave[1] * back[0])

    grad = jnp.stack([v.astype(BF) for v in grad0 + grad1])
    grad = lax.dynamic_slice_in_dim(grad, core * 256, 256, axis=1)
    grad = grad.reshape(4, 32, 8, 4, 128).transpose(1, 3, 0, 2, 4).reshape(128, 32, 128)
    back_home = lax.all_to_all(grad, ALL, 0, 0, tiled=True)
    parts = back_home.reshape(64, 2, 4, 8, 128).transpose(0, 2, 1, 3, 4).reshape(64, 4, 16, 128).astype(F32)
    sums = []
    for a in range(2):
        for b in range(4):
            sums.append(jnp.sum(jnp.where((pick == 4 * a + b)[:, None], parts, 0.0), axis=0))
    sums = jnp.stack(sums).reshape(2, 4, 4, 16, 128).transpose(0, 3, 1, 2, 4).reshape(128, 4, 128)
    final = lax.all_to_all(sums.astype(BF), ALL, 0, 0, tiled=True)
    final = final.reshape(32, 4, 4, 128).transpose(2, 0, 1, 3).reshape(4, 32, 512)
    gradient = lax.dot_general(place, final, (((1,), (2,)), ((), ())), preferred_element_type=F32)
    gradient = gradient.transpose(1, 0, 2).reshape(2, 2, 512, 32)

    loss_other = lax.ppermute(loss[None], "tile", [(0, 2), (1, 3), (2, 0), (3, 1)])
    pair = jnp.concatenate([loss[None], loss_other])
    probe_losses = jnp.where(which == 0, pair, pair[::-1])
    return gradient, probe_losses


def solution(mesh):
    return jax.shard_map(
        body,
        mesh=mesh,
        in_specs=(
            P(None, None, "tile", "probe"),
            P(),
            P("probe", None, None),
            P("probe", None),
            P("probe"),
        ),
        out_specs=(P(None, None, "tile", "probe"), P("probe")),
        check_vma=False,
    )
```

profile of v0, /device:TPU:1, one launch (start us, length us, event | category | flops | bytes accessed | tf_op | source)
XLA Modules:
  0.0 133.1 jit_solution(15307036490196873541)
XLA Ops:
  0.7 0.9 fusion.81
  1.6 0.7 convert_bitcast_fusion.9
  3.2 0.8 pad_maximum_fusion
  4.0 11.5 %all-to-all-start = ((bf16[128,8,128]{2,1,0:T(8,128)(2,1)}), bf16[128,8,128]{2,1,0:T(8,128)(2,1)S(1)}, u32[]{:S(2)}, u32[]{:S(2)}) async-start(bf16[128,8,128]{2,1,0:T(8,128)(2,1)} %pad_maximum_fusion), calls=%async_computation | async-start | bytes 524288 | tf_op jit(solution)/shard_map/all_to_all | solution.py:88
  15.6 11.3 %all-to-all-done = bf16[128,8,128]{2,1,0:T(8,128)(2,1)S(1)} async-done(((bf16[128,8,128]{2,1,0:T(8,128)(2,1)}), bf16[128,8,128]{2,1,0:T(8,128)(2,1)S(1)}, u32[]{:S(2)}, u32[]{:S(2)}) %all-to-all-start) | async-done | bytes 262176 | tf_op jit(solution)/shard_map/all_to_all | solution.py:88
  27.8 0.7 add_compare_fusion.7
  28.6 2.1 %select_select_fusion = bf16[64,2,4,8,128]{4,3,2,1,0:T(8,128)(2,1)S(1)} fusion(pred[64,2,8,128]{3,2,1,0:T(8,128)(4,1)S(1)} %get-tuple-element.42, pred[64,2,8,128]{3,2,1,0:T(8,128)(4,1)S(1)} %get-tuple-element.43, pred[64,2,8,128]{3,2,1,0:T(8,128)(4,1)S(1)} %get-tuple-element.44, pred[64,2,8,128]{3,2,1,0:T(8,128)(4,1)S(1)} %get-tuple-element.45, ...), kind=kLoop, calls=%fused_computation.75 | loop fusion | flops 4194304 | bytes 2228224 | tf_op jit(solution)/shard_map/jit(_where)/select_n | solution.py:102
  30.6 23.0 %all_to_all.20 = bf16[128,32,128]{2,1,0:T(8,128)(2,1)S(1)} all-to-all(bf16[128,32,128]{2,1,0:T(8,128)(2,1)S(1)} %bitcast.271), channel_id=1, replica_groups=mesh['probe'=32,'tile'=4] {'probe','tile'}, dimensions={0} | all-to-all | bytes 2097152 | tf_op jit(solution)/shard_map/all_to_all | solution.py:104
  53.7 1.2 copy.184
  55.3 0.6 constant_dynamic-slice_fusion
  55.9 0.6 dynamic_slice.15
  56.4 1.3 add_select_fusion.2
  57.8 2.8 %fusion.22 = f32[512,512]{1,0:T(8,128)} fusion(s32[512]{0:T(512)S(1)} %get-tuple-element.56, bf16[2,512,512]{2,1,0:T(8,128)(2,1)} %param.10, s32[512]{0:T(512)S(1)} %get-tuple-element.57), kind=kOutput, calls=%fused_computation.63 | convolution fusion | flops 537657344 | bytes 1576960 | tf_op jit(solution)/shard_map/dot_general | solution.py:42
  60.7 2.5 %maximum_convert_fusion = f32[4,512,512]{2,1,0:T(8,128)} fusion(bf16[4,256,512]{2,1,0:T(8,128)(2,1)S(1)} %get-tuple-element.30, bf16[4,256,512]{2,1,0:T(8,128)(2,1)S(1)} %get-tuple-element.29), kind=kLoop, calls=%fused_computation.24 | loop fusion | flops 4194304 | bytes 6291456 | tf_op jit(solution)/shard_map/convert_element_type | solution.py:119
  63.2 3.9 %add_convert_fusion.4 = (bf16[512,512]{1,0:T(8,128)(2,1)S(1)}, bf16[512,512]{1,0:T(8,128)(2,1)S(1)}, f32[512,512]{1,0:T(8,128)}) fusion(f32[512,512]{1,0:T(8,128)} %fusion.22, f32[4,512,512]{2,1,0:T(8,128)} %maximum_convert_fusion, s32[512]{0:T(512)S(1)} %get-tuple-element.56, bf16[2,512,512]{2,1,0:T(8,128)(2,1)} %param.10, s32[512]{0:T(512)S(1)} %get-tuple-element.57), kind=kOutput, calls=%fused_computation.87 | convolution fusion | flops 539754496 | bytes 5771264 | tf_op jit(solution)/shard_map/dot_general | solution.py:42
  67.2 0.4 fusion.85
  67.6 0.6 copy-done.3
  68.2 0.4 fusion.84
  68.7 0.4 fusion.15
  69.1 0.4 fusion.14
  69.5 0.4 fusion.94
  70.0 0.4 fusion.95
  70.4 0.4 fusion.12
  70.9 1.3 copy-done.5
  72.2 0.7 add_convert_fusion.3
  73.2 0.4 fusion.88
  74.4 0.4 fusion.16
  74.8 0.5 fusion.87
  75.3 0.5 fusion.89
  75.7 0.4 fusion.17
  76.2 0.5 convolution_subtract_fusion.1
  76.7 1.1 copy-done.8
  77.8 1.3 multiply_reduce_fusion
  79.5 0.5 fusion.92
  80.0 0.5 fusion.90
  80.4 0.5 fusion.18
  80.9 0.5 convolution_negate_fusion.2
  81.4 0.5 fusion.91
  81.9 0.5 fusion.19
  82.4 0.5 convolution_add_fusion.4
  82.9 0.5 convolution_add_fusion.5
  83.3 1.0 fusion.35
  84.3 0.4 convolution_negate_fusion.1
  84.8 0.4 fusion.93
  85.2 0.4 fusion.21
  85.6 0.4 fusion.97
  86.1 0.4 fusion.20
  86.5 0.6 fusion.96
  87.2 0.4 fusion.9
  87.6 0.4 fusion.10
  88.1 0.8 copy-done.6
  89.1 0.6 fusion.33
  89.8 1.3 copy.116
  91.1 3.6 %all-to-all-start.2 = ((bf16[128,32,128]{2,1,0:T(8,128)(2,1)}), bf16[128,32,128]{2,1,0:T(8,128)(2,1)S(1)}, u32[]{:S(2)}, u32[]{:S(2)}) async-start(bf16[128,32,128]{2,1,0:T(8,128)(2,1)} %bitcast.44), calls=%async_computation.2 | async-start | bytes 2097152 | tf_op jit(solution)/shard_map/all_to_all | solution.py:140
  95.3 2.4 %collective-permute-start.1 = (f32[1]{0:T(128)}, f32[1]{0:T(128)}, u32[]{:S(2)}, u32[]{:S(2)}) collective-permute-start(f32[1]{0:T(128)} %bitcast.70), channel_id=1, source_target_pairs={{0,2},{1,3},{2,0},{3,1},{4,6},{5,7},{6,4},{7,5},{8,10},{9,11},{10,... | collective-permute-start | bytes 20 | tf_op jit(solution)/shard_map/ppermute | solution.py:152
  97.7 0.5 collective-permute-done.1
  98.3 0.6 pad_maximum_fusion.2
  99.0 15.1 %all-to-all-done.2 = bf16[128,32,128]{2,1,0:T(8,128)(2,1)S(1)} async-done(((bf16[128,32,128]{2,1,0:T(8,128)(2,1)}), bf16[128,32,128]{2,1,0:T(8,128)(2,1)S(1)}, u32[]{:S(2)}, u32[]{:S(2)}) %all-to-all-start.2) | async-done | bytes 1048608 | tf_op jit(solution)/shard_map/all_to_all | solution.py:140
  114.1 2.4 %fusion.7 = (bf16[2,4,8,128]{3,2,1,0:T(8,128)(2,1)S(1)}, bf16[2,4,8,128]{3,2,1,0:T(8,128)(2,1)S(1)}, bf16[2,4,8,128]{3,2,1,0:T(8,128)(2,1)S(1)}, bf16[2,4,8,128]...) fusion(bf16[64,2,4,8,128]{4,3,2,1,0:T(8,128)(2,1)S(1)} %bitcast, ...), kind=kLoop, calls=%fused_computation.23 | loop fusion | flops 8847360 | bytes 2228224 | tf_op jit(solution)/shard_map/reduce_sum | solution.py:145
  116.7 0.8 copy.126
  117.5 4.2 %all-to-all-start.3 = ((bf16[128,4,128]{2,1,0:T(4,128)(2,1)}), bf16[128,4,128]{2,1,0:T(4,128)(2,1)S(1)}, u32[]{:S(2)}, u32[]{:S(2)}) async-start(bf16[128,4,128]{2,1,0:T(4,128)(2,1)} %copy.126), calls=%async_computation.3 | async-start | bytes 262144 | tf_op jit(solution)/shard_map/all_to_all | solution.py:147
  121.7 1.1 broadcast_select_fusion.2
  122.9 9.1 %all-to-all-done.3 = bf16[128,4,128]{2,1,0:T(4,128)(2,1)S(1)} async-done(((bf16[128,4,128]{2,1,0:T(4,128)(2,1)}), bf16[128,4,128]{2,1,0:T(4,128)(2,1)S(1)}, u32[]{:S(2)}, u32[]{:S(2)}) %all-to-all-start.3) | async-done | bytes 131104 | tf_op jit(solution)/shard_map/all_to_all | solution.py:147
  132.0 1.1 fusion.30
  (59 shorter events, 4.6 us)
Async XLA Ops:
  0.6 2.0 %copy-start = (bf16[2,2,512,32]{2,3,1,0:T(8,128)(2,1)S(1)}, bf16[2,2,512,32]{2,3,1,0:T(8,128)(2,1)}, u32[]{:S(2)}) copy-start(bf16[2,2,512,32]{2,3,1,0:T(8,128)(2,1)} %param.9) | copy-start | bytes 393220
  4.0 22.9 %all-to-all-start = ((bf16[128,8,128]{2,1,0:T(8,128)(2,1)}), bf16[128,8,128]{2,1,0:T(8,128)(2,1)S(1)}, u32[]{:S(2)}, u32[]{:S(2)}) async-start(bf16[128,8,128]{2,1,0:T(8,128)(2,1)} %pad_maximum_fusion), calls=%async_computation | async-start | bytes 524288 | tf_op jit(solution)/shard_map/all_to_all | solution.py:88
  54.9 5.7 %collective-permute-start = (bf16[4,256,512]{2,1,0:T(8,128)(2,1)}, bf16[4,256,512]{2,1,0:T(8,128)(2,1)S(1)}, u32[]{:S(2)}, u32[]{:S(2)}) collective-permute-start(bf16[4,256,512]{2,1,0:T(8,128)(2,1)} %bitcast.265), channel_id=1, source_target_pairs={{0,1},{1,0},{2,3},{3,2},{4,5},{5,4},{6,7},{7,6},{8,9},{9,8},{10,11... | collective-permute-start | bytes 3145736 | tf_op jit(solution)/shard_map/ppermute | solution.py:107
  63.2 3.9 %copy-start.1 = (bf16[512,512]{1,0:T(8,128)(2,1)S(1)}, bf16[512,512]{1,0:T(8,128)(2,1)}, u32[]{:S(2)}) copy-start(bf16[512,512]{1,0:T(8,128)(2,1)} %constant.271.clone) | copy-start | bytes 1572868
  67.2 1.0 copy-start.3
  70.0 2.2 %copy-start.5 = (f32[4,512,512]{2,1,0:T(8,128)S(1)}, f32[4,512,512]{2,1,0:T(8,128)}, u32[]{:S(2)}) copy-start(f32[4,512,512]{2,1,0:T(8,128)} %maximum_convert_fusion) | copy-start | bytes 12582916
  72.2 1.0 copy-start.2
  72.8 1.1 copy-start.4
  76.2 1.6 %copy-start.8 = (f32[2,512,512]{2,1,0:T(8,128)S(1)}, f32[2,512,512]{2,1,0:T(8,128)}, u32[]{:S(2)}) copy-start(f32[2,512,512]{2,1,0:T(8,128)} %param.11) | copy-start | bytes 6291460
  87.6 1.2 copy-start.6
  87.6 1.5 %copy-start.7 = (f32[512,512]{1,0:T(8,128)S(1)}, f32[512,512]{1,0:T(8,128)}, u32[]{:S(2)}) copy-start(f32[512,512]{1,0:T(8,128)} %get-tuple-element.53) | copy-start | bytes 3145732
  91.1 23.0 %all-to-all-start.2 = ((bf16[128,32,128]{2,1,0:T(8,128)(2,1)}), bf16[128,32,128]{2,1,0:T(8,128)(2,1)S(1)}, u32[]{:S(2)}, u32[]{:S(2)}) async-start(bf16[128,32,128]{2,1,0:T(8,128)(2,1)} %bitcast.44), calls=%async_computation.2 | async-start | bytes 2097152 | tf_op jit(solution)/shard_map/all_to_all | solution.py:140
  95.3 2.9 %collective-permute-start.1 = (f32[1]{0:T(128)}, f32[1]{0:T(128)}, u32[]{:S(2)}, u32[]{:S(2)}) collective-permute-start(f32[1]{0:T(128)} %bitcast.70), channel_id=1, source_target_pairs={{0,2},{1,3},{2,0},{3,1},{4,6},{5,7},{6,4},{7,5},{8,10},{9,11},{10,... | collective-permute-start | bytes 20 | tf_op jit(solution)/shard_map/ppermute | solution.py:152
  117.5 14.4 %all-to-all-start.3 = ((bf16[128,4,128]{2,1,0:T(4,128)(2,1)}), bf16[128,4,128]{2,1,0:T(4,128)(2,1)S(1)}, u32[]{:S(2)}, u32[]{:S(2)}) async-start(bf16[128,4,128]{2,1,0:T(4,128)(2,1)} %copy.126), calls=%async_computation.3 | async-start | bytes 262144 | tf_op jit(solution)/shard_map/all_to_all | solution.py:147
where the time goes:
time: 134 us; the launch traced here: 133 us
  waiting for transfers between devices  36 us (27%)
  matrix products  23.7 us (18%)
  blocking collectives  23 us (17%)
  starting transfers between devices  22.1 us (16%)
  other arithmetic  15.1 us (11%)
  local copies, waits for them, and re-layouts  11.3 us (8%)
  between operations  1.78 us (1%)
    all_to_all x1, blocking collectives, body(): mine = lax.all_to_all(sent, ALL, 0, 0, tiled=True)  23 us
    dot_general x34, matrix products, dot(): lax.dot_general(left, right, (dims, ((), ())), preferred_element_type=F32)  22.4 us
    all_to_all x1, waiting for transfers between devices, body(): back_home = lax.all_to_all(grad, ALL, 0, 0, tiled=True)  15.1 us
    all_to_all x1, starting transfers between devices, body(): lax.all_to_all(jnp.concatenate([block, info], axis=1), ALL, 0, 0, tiled=T...  11.5 us
    all_to_all x1, waiting for transfers between devices, body(): lax.all_to_all(jnp.concatenate([block, info], axis=1), ALL, 0, 0, tiled=T...  11.3 us
    all_to_all x1, waiting for transfers between devices, body(): final = lax.all_to_all(sums.astype(BF), ALL, 0, 0, tiled=True)  9.06 us
    unnamed x27, local copies, waits for them, and re-layouts  4.95 us
    all_to_all x1, starting transfers between devices, body(): final = lax.all_to_all(sums.astype(BF), ALL, 0, 0, tiled=True)  4.23 us
  transfers between devices with their start and end apart: 5, of which 4 were waited for; matrix products, arithmetic and copies ran while one was open for 5% of the time, Pallas kernels for 0%

commit v1 on v0

v1 whole, which is shorter than its diff:
```python
import math

import jax
import jax.numpy as jnp
import numpy as np
from jax import lax
from jax.experimental import pallas as pl
from jax.experimental.pallas import tpu as pltpu
from jax.sharding import Mesh
from jax.sharding import PartitionSpec as P

FRAME = 512
BORDER = 128
TILE_ROWS = 512
FRESNEL = 0.25
PROBE = ("half", "col")
CHIPS = ("half", "col", "zl")
ALL = ("half", "col", "zl", "core")
SHARERS = ("half", "zl", "core")
BF = jnp.bfloat16
F32 = jnp.float32


def natural(order):
    return order % 16 * 32 + order // 16


def build_tables():
    n = FRAME
    index = np.arange(n)
    angle = (np.float32(-2.0 * math.pi) * (np.outer(index, index) % n).astype(np.float32) / np.float32(n)).astype(np.float32)
    norm = np.float32(1.0 / math.sqrt(n))
    wave_re, wave_im = np.cos(angle) * norm, np.sin(angle) * norm
    freq = np.where(index < n // 2, index, index - n).astype(np.float32)
    phase = (np.float32(-math.pi * FRESNEL) * freq * freq / np.float32(n)).astype(np.float32)
    kre, kim = np.cos(phase)[:, None], np.sin(phase)[:, None]
    sre, sim = kre * wave_re - kim * wave_im, kre * wave_im + kim * wave_re
    prop_re = wave_re @ sre + wave_im @ sim
    prop_im = wave_re @ sim - wave_im @ sre
    perm = natural(index)
    bf = jnp.bfloat16
    far = (wave_re[perm].astype(bf), wave_im[perm].astype(bf))
    prop = (prop_re[perm][:, perm].astype(bf), prop_im[perm][:, perm].astype(bf))
    return far, prop


def right_form(re, im):
    re, im = jnp.asarray(re), jnp.asarray(im)
    return jnp.concatenate([jnp.concatenate([re, im], 1), jnp.concatenate([-im, re], 1)], 0)


def dot(left, right, dims):
    return lax.dot_general(left, right, (dims, ((), ())), preferred_element_type=F32)


NN = ((1,), (0,))
NT = ((1,), (1,))


def probe_kernel(
    core_ref, own, other, wave, measured_hbm, bq_hbm, aq_hbm, bw_hbm, aw_hbm, out, loss,
    y, inner, x1, field, turn, measured, bq, aq, bw, aw, sems,
):
    copies = [
        pltpu.make_async_copy(src, dst, sems.at[n])
        for n, (src, dst) in enumerate(
            ((bq_hbm, bq), (aq_hbm, aq), (bw_hbm, bw), (aw_hbm, aw), (measured_hbm, measured))
        )
    ]
    for copy in copies:
        copy.start()
    core = core_ref[0]
    first = core == 0
    here = pl.multiple_of(core * 256, 256)

    def layer(i, z, c, plane):
        mine, rest = own[i, z, c, plane].astype(F32), other[i, z, c, plane].astype(F32)
        return jnp.concatenate([jnp.where(first, mine, rest), jnp.where(first, rest, mine)], axis=0)

    def block_rows(i):
        return pl.ds(pl.multiple_of(i * 16, 16), 16), pl.ds(pl.multiple_of(512 + i * 16, 16), 16)

    def product(plane, get, conj):
        def step(i, _):
            rows, _ = block_rows(i)
            for z in range(2):
                for c in range(2):
                    at = 256 * c + 128 * z
                    ore, oim = layer(i, z, c, plane), layer(i, z, c, plane + 1)
                    vre, vim = get(i, slice(at, at + 128))
                    if conj:
                        re, im = ore * vre + oim * vim, ore * vim - oim * vre
                    else:
                        re, im = ore * vre - oim * vim, ore * vim + oim * vre
                    y[rows, at : at + 128] = re.astype(BF)
                    y[rows, 512 + at : 640 + at] = im.astype(BF)
            return 0

        lax.fori_loop(0, 32, step, 0, unroll=2)

    def from_wave(i, lanes):
        rows, _ = block_rows(i)
        return wave[0, rows, lanes].astype(F32), wave[1, rows, lanes].astype(F32)

    def from_ref(ref):
        def get(i, lanes):
            rows, rows_im = block_rows(i)
            return ref[rows, lanes], ref[rows_im, lanes]

        return get

    def right(table):
        for n in range(4):
            got = jnp.dot(y[...], table[:, n * 256 : n * 256 + 256], preferred_element_type=F32)
            inner[n // 2 * 512 : n // 2 * 512 + 512, n % 2 * 256 : n % 2 * 256 + 256] = got.astype(BF)

    def left(table, dst):
        for n in range(2):
            dst[:, n * 256 : n * 256 + 256] = jnp.dot(
                table[...], inner[:, n * 256 : n * 256 + 256], preferred_element_type=F32
            )

    def hand_out(plane):
        for o in range(4):
            for j in range(16):
                for part in range(2):
                    rows = pl.ds(part * 512 + 128 * o + j, 8, stride=16)
                    for z in range(2):
                        out[o // 2, j, o % 2, z, plane + part] = turn[z, rows, :].astype(BF)

    product(0, from_wave, False)
    copies[0].wait()
    right(bq)
    copies[1].wait()
    left(aq, x1)
    product(2, from_ref(x1), False)
    copies[2].wait()
    right(bw)
    copies[3].wait()
    left(aw, field)
    copies[4].wait()

    def compare(i, total):
        rows, rows_im = block_rows(i)
        re, im = field[rows, :], field[rows_im, :]
        misfit = re * re + im * im - measured[rows, :]
        y[rows, 0:512] = (misfit * re).astype(BF)
        y[rows, 512:1024] = (misfit * im).astype(BF)
        return total + misfit * misfit

    total = lax.fori_loop(0, 32, compare, jnp.zeros((16, 512), F32))
    loss[...] = jnp.full((8, 128), jnp.sum(total) * (1.0 / (FRAME * FRAME)), F32)
    right(aw)
    left(bw, field)
    product(2, from_ref(field), True)

    def gradient1(i, _):
        rows, rows_im = block_rows(i)
        for z in range(2):
            lanes = pl.ds(pl.multiple_of(here + z * 128, 128), 128)
            bre, bim = field[rows, lanes], field[rows_im, lanes]
            xre, xim = x1[rows, lanes], x1[rows_im, lanes]
            turn[z, rows, :] = xre * bre + xim * bim
            turn[z, rows_im, :] = xre * bim - xim * bre
        return 0

    lax.fori_loop(0, 32, gradient1, 0, unroll=2)
    hand_out(2)
    for part in range(2):
        cols = pl.ds(pl.multiple_of(here + part * 512, 256), 256)
        got = jnp.dot(y[...], aq[:, cols], preferred_element_type=F32)
        inner[part * 512 : part * 512 + 512, 0:256] = got.astype(BF)
    field[:, 0:256] = jnp.dot(bq[...], inner[:, 0:256], preferred_element_type=F32)

    def gradient0(i, _):
        rows, rows_im = block_rows(i)
        for z in range(2):
            bre, bim = field[rows, z * 128 : z * 128 + 128], field[rows_im, z * 128 : z * 128 + 128]
            xre, xim = from_wave(i, pl.ds(pl.multiple_of(here + z * 128, 128), 128))
            turn[z, rows, :] = xre * bre + xim * bim
            turn[z, rows_im, :] = xre * bim - xim * bre
        return 0

    lax.fori_loop(0, 32, gradient0, 0, unroll=2)
    hand_out(0)


VM = pl.BlockSpec(memory_space=pltpu.VMEM)
SM = pl.BlockSpec(memory_space=pltpu.SMEM)
ANY = pl.BlockSpec(memory_space=pl.ANY)
PARAMS = pltpu.CompilerParams(vmem_limit_bytes=56 * 2**20)


def probe_step(core, own, other, wave, measured, tables):
    return pl.pallas_call(
        probe_kernel,
        out_shape=(
            jax.ShapeDtypeStruct((2, 16, 2, 2, 4, 8, 128), BF),
            jax.ShapeDtypeStruct((8, 128), F32),
        ),
        in_specs=[SM, VM, VM, VM] + [ANY] * 5,
        out_specs=(VM, VM),
        scratch_shapes=[
            pltpu.VMEM((512, 1024), BF),
            pltpu.VMEM((1024, 512), BF),
            pltpu.VMEM((1024, 512), F32),
            pltpu.VMEM((1024, 512), F32),
            pltpu.VMEM((2, 1024, 128), F32),
            pltpu.VMEM((512, 512), F32),
        ]
        + [pltpu.VMEM((1024, 1024), BF)] * 4
        + [pltpu.SemaphoreType.DMA((5,))],
        compiler_params=PARAMS,
        name="probe_step",
    )(core.reshape(1), own, other, wave, measured, *tables)


def roll_kernel(meta, illumination, intensities, wave, measured, raw, sem):
    copy = pltpu.make_async_copy(intensities.at[meta[2]], raw, sem)
    copy.start()
    at0 = lax.broadcasted_iota(jnp.int32, (FRAME, FRAME), 0)
    at1 = lax.broadcasted_iota(jnp.int32, (FRAME, FRAME), 1)
    cols = jnp.where(((natural(at0) - meta[1]) & (FRAME - 1)) == at1, 1.0, 0.0).astype(BF)
    rows = jnp.where(((natural(at1) - meta[0]) & (FRAME - 1)) == at0, 1.0, 0.0).astype(BF)
    for part in range(2):
        turned = lax.dot_general(cols, illumination[part], (NT, ((), ())), preferred_element_type=F32)
        wave[part] = jnp.dot(turned.astype(BF), rows, preferred_element_type=F32).astype(BF)
    copy.wait()
    measured[...] = raw[...].T


def roll_step(meta, illumination, intensities):
    return pl.pallas_call(
        roll_kernel,
        out_shape=(
            jax.ShapeDtypeStruct((2, FRAME, FRAME), BF),
            jax.ShapeDtypeStruct((FRAME, FRAME), F32),
        ),
        in_specs=[SM, VM, ANY],
        out_specs=(VM, VM),
        scratch_shapes=[pltpu.VMEM((FRAME, FRAME), F32), pltpu.SemaphoreType.DMA],
        compiler_params=PARAMS,
        name="roll_step",
    )(meta, illumination, intensities)


def sum_kernel(meta, parts, out, acc):
    core, base = meta[128], meta[129]
    acc[...] = jnp.zeros(acc.shape, F32)
    at0 = lax.broadcasted_iota(jnp.int32, (8, 128), 0)
    at1 = lax.broadcasted_iota(jnp.int32, (8, 128), 1)
    column = base + at0
    row = [natural(256 * c + 128 * core + at1) for c in range(2)]

    def step(k, _):
        top, edge = meta[k] >> 9, meta[k] & (FRAME - 1)
        right = column < meta[64 + k]
        for c in range(2):
            below = row[c] < edge
            for plane in range(4):
                g = parts[k, c, plane].astype(F32)
                for tile, piece in ((top, jnp.where(below, 0.0, g)), (top + 1, jnp.where(below, g, 0.0))):
                    acc[0, tile, plane, c] += jnp.where(right, 0.0, piece)
                    acc[1, tile, plane, c] += jnp.where(right, piece, 0.0)
        return 0

    lax.fori_loop(0, 64, step, 0)
    for h in range(2):
        for tile in range(4):
            for plane in range(4):
                for c in range(2):
                    out[4 * h + tile, plane, :, 128 * c : 128 * c + 128] = acc[h, tile, plane, c].astype(BF)


def sum_step(meta, parts):
    return pl.pallas_call(
        sum_kernel,
        out_shape=jax.ShapeDtypeStruct((8, 4, 8, 256), BF),
        in_specs=[SM, VM],
        out_specs=VM,
        scratch_shapes=[pltpu.VMEM((2, 5, 4, 2, 8, 128), F32)],
        compiler_params=PARAMS,
        name="sum_step",
    )(meta, parts)


def body(transmission, illumination, intensities, scan_positions, tile_owner):
    (far_re, far_im), (prop_re, prop_im) = build_tables()
    half, col = lax.axis_index("half"), lax.axis_index("col")
    which, core = lax.axis_index("zl"), lax.axis_index("core")
    my_col = half * 16 + col
    order = jnp.arange(FRAME, dtype=jnp.int32)
    residue = natural(order)

    row0 = tile_owner * TILE_ROWS - BORDER + scan_positions[:, 0]
    col0 = scan_positions[:, 1]
    info = jnp.stack([row0 // 32, row0 % 32, col0 // 32, col0 % 32], axis=1).reshape(8).astype(BF)
    place = (residue[None, :] == order[:, None]).astype(BF)
    block = dot(transmission.reshape(4, 512, 32), place, ((1,), (0,))).astype(BF)
    block = block.reshape(4, 32, 2, 2, 128).transpose(1, 3, 2, 0, 4).reshape(128, 4, 128)
    info = jnp.broadcast_to(jnp.pad(info, (0, 120)), (128, 4, 128))
    got = lax.all_to_all(jnp.concatenate([block, info], axis=1), ALL, 0, 0, tiled=True)

    mine = jnp.stack([row0, col0], axis=1)[which]
    wave, measured = roll_step(jnp.concatenate([mine, which.reshape(1)]), illumination, intensities)
    tables = (
        right_form(prop_re, prop_im),
        right_form(prop_re, -prop_im),
        right_form(far_re, far_im),
        right_form(far_re.T, -far_im.T),
    )
    got, wave, measured = lax.optimization_barrier((got, wave, measured))

    told = got[::4, 4, :8].astype(jnp.int32).reshape(64, 4)
    rows0 = told[:, 0] * 32 + told[:, 1]
    cols0 = told[:, 2] * 32 + told[:, 3]
    cand = got[:, :4].reshape(2, 2, 8, 4, 4, 128).transpose(0, 3, 1, 4, 2, 5)
    column = (jnp.arange(16, dtype=jnp.int32) * 32 + my_col).reshape(2, 8)
    row = natural((2 * core + which) * 128 + jnp.arange(128, dtype=jnp.int32))
    side = (column[None] < cols0[:, None, None]).astype(jnp.int32)
    tile = rows0[:, None] // 512 + (row[None, :] < rows0[:, None] % 512)
    pick = tile[:, None, None, :] + 4 * side[..., None]
    sent = jnp.zeros((64, 2, 4, 8, 128), BF)
    for a in range(2):
        for b in range(4):
            sent = jnp.where((pick == 4 * a + b)[:, :, None], cand[a, b][None], sent)
    own = lax.all_to_all(sent.reshape(128, 4, 8, 128), ALL, 0, 0, tiled=True).reshape(32, 2, 2, 4, 8, 128)
    other = lax.ppermute(own, "core", [(0, 1), (1, 0)])

    grad, loss = probe_step(core, own, other, wave, measured, tables)

    home = lax.all_to_all(grad.reshape(128, 4, 8, 128), ALL, 0, 0, tiled=True)
    base = col * 32 + (half * 2 + which) * 8
    sums = sum_step(jnp.concatenate([rows0, cols0, jnp.stack([core, base])]), home.reshape(64, 2, 4, 8, 128))
    final = lax.all_to_all(sums, SHARERS, 0, 0, tiled=True)
    final = final.reshape(2, 2, 2, 4, 8, 2, 128).transpose(3, 0, 1, 4, 5, 2, 6).reshape(4, 32, 512)
    gradient = lax.dot_general(place, final, (((1,), (2,)), ((), ())), preferred_element_type=F32)
    gradient = gradient.transpose(1, 0, 2).reshape(2, 2, 512, 32)

    loss = loss[0, :1]
    loss_other = lax.ppermute(loss, "zl", [(0, 1), (1, 0)])
    pair = jnp.concatenate([loss, loss_other])
    probe_losses = jnp.where(which == 0, pair, pair[::-1])
    return gradient, probe_losses


def solution(mesh):
    split = Mesh(mesh.devices.reshape(2, 16, 2, 2), ALL)
    tile = ("zl", "core")
    return jax.shard_map(
        body,
        mesh=split,
        in_specs=(
            P(None, None, tile, PROBE),
            P(),
            P(PROBE, None, None),
            P(PROBE, None),
            P(PROBE),
        ),
        out_specs=(P(None, None, tile, PROBE), P(PROBE)),
        check_vma=False,
    )
```

time: 134 us -> 112 us (0.84)
  Pallas kernels: 0 us -> 24.1 us
  matrix products: 23.7 us -> 1.38 us
  waiting for transfers between devices: 36 us -> 27.3 us
  other arithmetic: 15.1 us -> 7.29 us
  local copies, waits for them, and re-layouts: 11.3 us -> 6.39 us
    pallas_call x0 -> x3, Pallas kernels: none -> 24.1 us  [the longest x1 17.1 us: probe_step(): pl.pallas_call(probe_kernel, out_shape=(jax.ShapeDtypeStruct((2, 16, 2, 2...]
    dot_general x34 -> x0, matrix products: 22.4 us -> none  [dot(): lax.dot_general(left, right, (dims, ((), ())), preferred_element_type=F32)]
    all_to_all x2, waiting for transfers between devices: 24.2 us -> 13 us  [the longest x1 9.07 us: body(): home = lax.all_to_all(grad.reshape(128, 4, 8, 128), ALL, 0, 0, tiled=True)]
    ppermute x2, waiting for transfers between devices: 0.54 us -> 7.64 us  [the longest x1 5.36 us: body(): loss_other = lax.ppermute(loss, 'zl', [(0, 1), (1, 0)])]
    all_to_all x1, waiting for transfers between devices: 11.3 us -> 6.62 us  [body(): lax.all_to_all(jnp.concatenate([block, info], axis=1), ALL, 0, 0, tiled=T...]
    convert_element_type x2 -> x0, other arithmetic: 2.93 us -> none  [the longest x1 2.52 us: body(): layer = patch.astype(F32)]
    unnamed x27 -> x9, local copies, waits for them, and re-layouts: 4.95 us -> 2.04 us
    select_n x3 -> x1, other arithmetic: 3.53 us -> 0.82 us  [body(): sent = jnp.where((pick == 4 * a + b)[:, :, None], cand[a, b][None], sent)]
  transfers between devices with their start and end apart: 5 -> 5, of which waited for: 4 -> 5; matrix products, arithmetic and copies ran while one was open for 5% -> 5% of each run, Pallas kernels for 0% -> 4%
where the time goes in v1:
time: 112 us; the launch traced here: 111 us
  waiting for transfers between devices  27.3 us (24%)
  Pallas kernels  24.1 us (22%)
  blocking collectives  23 us (21%)
  starting transfers between devices  21 us (19%)
  other arithmetic  7.29 us (7%)
  local copies, waits for them, and re-layouts  6.39 us (6%)
  matrix products  1.38 us (1%)
    all_to_all x1, blocking collectives, body(): lax.all_to_all(sent.reshape(128, 4, 8, 128), ALL, 0, 0, tiled=True)  23 us
    pallas_call x1, Pallas kernels, probe_step(): pl.pallas_call(probe_kernel, out_shape=(jax.ShapeDtypeStruct((2, 16, 2, 2...  17.1 us
    all_to_all x1, starting transfers between devices, body(): lax.all_to_all(jnp.concatenate([block, info], axis=1), ALL, 0, 0, tiled=T...  11.5 us
    all_to_all x1, waiting for transfers between devices, body(): home = lax.all_to_all(grad.reshape(128, 4, 8, 128), ALL, 0, 0, tiled=True)  9.07 us
    all_to_all x1, waiting for transfers between devices, body(): lax.all_to_all(jnp.concatenate([block, info], axis=1), ALL, 0, 0, tiled=T...  6.62 us
    ppermute x1, waiting for transfers between devices, body(): loss_other = lax.ppermute(loss, 'zl', [(0, 1), (1, 0)])  5.36 us
    all_to_all x1, waiting for transfers between devices, body(): final = lax.all_to_all(sums, SHARERS, 0, 0, tiled=True)  3.94 us
    pallas_call x1, Pallas kernels, roll_step(): pl.pallas_call(roll_kernel, out_shape=(jax.ShapeDtypeStruct((2, FRAME, FR...  3.91 us
  transfers between devices with their start and end apart: 5, of which 5 were waited for; matrix products, arithmetic and copies ran while one was open for 5% of the time, Pallas kernels for 4%

profile of v1, /device:TPU:1, one launch (start us, length us, event | category | flops | bytes accessed | tf_op | source)
XLA Modules:
  0.0 111.3 jit_solution(5465549774210921046)
XLA Ops:
  0.6 0.0 copy-start
  0.7 0.9 slice_reduce_fusion
  1.6 0.1 copy.55
  1.7 0.7 convert_bitcast_fusion.1
  2.4 0.1 copy.43
  2.5 0.1 convert_element_type.31
  2.6 0.0 copy-done
  2.6 0.3 fusion.8
  3.0 0.1 copy.41
  3.2 0.9 copy.44
  4.1 11.5 %all-to-all-start = ((bf16[128,8,128]{2,1,0:T(8,128)(2,1)}), bf16[128,8,128]{2,1,0:T(8,128)(2,1)S(1)}, u32[]{:S(2)}, u32[]{:S(2)}) async-start(bf16[128,8,128]{2,1,0:T(8,128)(2,1)} %copy.44), calls=%async_computation | async-start | bytes 524288 | tf_op jit(solution)/shard_map/all_to_all | solution.py:302
  15.6 0.2 dynamic-slice_reduce_fusion
  15.8 0.6 pad_add_fusion.2.meta
  16.4 3.9 %roll_step.1 = (bf16[2,512,512]{2,1,0:T(8,128)(2,1)}, f32[512,512]{1,0:T(8,128)}) custom-call(s32[3]{0:T(128)} %pad_add_fusion.2.meta, bf16[2,512,512]{2,1,0:T(8,128)(2,1)} %illumination.1, f32[2,512,512]{2,1,0:T(8,128)} %intensities.1), custom_call_target="tpu_custom_call" | custom-call | tf_op jit(solution)/shard_map/roll_step/pallas_call | solution.py:233
  20.3 6.6 %all-to-all-done = bf16[128,8,128]{2,1,0:T(8,128)(2,1)S(1)} async-done(((bf16[128,8,128]{2,1,0:T(8,128)(2,1)}), bf16[128,8,128]{2,1,0:T(8,128)(2,1)S(1)}, u32[]{:S(2)}, u32[]{:S(2)}) %all-to-all-start) | async-done | bytes 262176 | tf_op jit(solution)/shard_map/all_to_all | solution.py:302
  26.9 0.1 convert_reduce_fusion
  27.1 0.1 reshape.259
  27.1 0.2 fusion.14
  27.4 0.1 lt.88
  27.5 0.1 lt.89
  27.6 0.2 fusion.34
  27.8 0.1 compare_select_fusion
  28.0 0.1 convert_add_fusion
  28.1 0.7 add_compare_fusion.7
  28.8 0.8 fusion.6
  29.6 23.0 %all_to_all.20 = bf16[128,4,8,128]{3,2,1,0:T(8,128)(2,1)S(1)} all-to-all(bf16[128,4,8,128]{3,2,1,0:T(8,128)(2,1)S(1)} %fusion.6), channel_id=1, replica_groups=mesh['half'=2,'col'=16,'zl'=2,'core'=2] {'half','col','zl','core'}, dimensions={0} | all-to-all | bytes 2097152 | tf_op jit(solution)/shard_map/all_to_all | solution.py:327
  52.7 0.0 copy-start.1
  52.7 0.4 collective-permute-start
  53.1 2.3 %collective-permute-done.other = bf16[32,2,2,4,8,128]{5,4,3,2,1,0:T(8,128)(2,1)S(1)} collective-permute-done((bf16[32,2,2,4,8,128]{5,4,3,2,1,0:T(8,128)(2,1)S(1)}, bf16[32,2,2,4,8,128]{5,4,3,2,1,0:T(8,128)(2,1)S(1)}, u32[]{:S(2)}, u32[]{:S(2)}) %collective-permute-start) | collective-permute-done | bytes 1048608 | tf_op jit(solution)/shard_map/ppermute | solution.py:328
  55.4 0.0 copy-start.3
  55.4 0.0 copy-done.1
  55.4 1.0 copy-done.3
  56.4 17.1 %probe_step.1 = (bf16[2,16,2,2,4,8,128]{6,5,4,3,2,1,0:T(8,128)(2,1)}, f32[8,128]{1,0:T(8,128)}) custom-call(s32[1]{0:T(128)} %bitcast.12.core_ref, bf16[32,2,2,4,8,128]{5,4,3,2,1,0:T(8,128)(2,1)} %bitcast.88, bf16[32,2,2,4,8,128]{5,4,3,2,1,0:T(8,128)(2,1)} %copy-done.3, bf16[2,512,512]{2,1,0:T(8,128)(2,1)} %get-tuple-element.12.wave, ...), custom_call_target="tpu_custom_call" | custom-call | tf_op jit(solution)/shard_map/probe_step/pallas_call | solution.py:195
  73.4 3.8 %all-to-all-start.2 = ((bf16[128,4,8,128]{3,2,1,0:T(8,128)(2,1)}), bf16[128,4,8,128]{3,2,1,0:T(8,128)(2,1)S(1)}, u32[]{:S(2)}, u32[]{:S(2)}) async-start(bf16[128,4,8,128]{3,2,1,0:T(8,128)(2,1)} %bitcast.91), calls=%async_computation.2 | async-start | bytes 2097152 | tf_op jit(solution)/shard_map/all_to_all | solution.py:332
  77.3 0.7 pad_add_fusion.1.meta
  77.9 1.3 %slice.67 = f32[1,1]{1,0:T(1,128)} slice(f32[8,128]{1,0:T(8,128)} %get-tuple-element.15), slice={[0:1], [0:1]} | slice | bytes 8 | tf_op jit(solution)/shard_map/slice | solution.py:340
  79.2 1.6 %collective-permute-start.1 = (f32[1]{0:T(128)}, f32[1]{0:T(128)}, u32[]{:S(2)}, u32[]{:S(2)}) collective-permute-start(f32[1]{0:T(128)} %bitcast.43), channel_id=1, source_target_pairs={{0,2},{2,0},{1,3},{3,1},{4,6},{6,4},{5,7},{7,5},{8,10},{10,8},{9,1... | collective-permute-start | bytes 20 | tf_op jit(solution)/shard_map/ppermute | solution.py:341
  80.8 5.4 %collective-permute-done.1 = f32[1]{0:T(128)} collective-permute-done((f32[1]{0:T(128)}, f32[1]{0:T(128)}, u32[]{:S(2)}, u32[]{:S(2)}) %collective-permute-start.1) | collective-permute-done | bytes 36 | tf_op jit(solution)/shard_map/ppermute | solution.py:341
  86.2 1.4 %pad_maximum_fusion.2 = f32[2]{0:T(128)S(1)} fusion(f32[1]{0:T(128)} %collective-permute-done.1, f32[1]{0:T(128)} %bitcast.43), kind=kLoop, calls=%fused_computation.91 | loop fusion | flops 2 | bytes 16 | tf_op jit(solution)/shard_map/concatenate | solution.py:342
  87.5 0.1 rev.3
  87.6 9.1 %all-to-all-done.2 = bf16[128,4,8,128]{3,2,1,0:T(8,128)(2,1)S(1)} async-done(((bf16[128,4,8,128]{3,2,1,0:T(8,128)(2,1)}), bf16[128,4,8,128]{3,2,1,0:T(8,128)(2,1)S(1)}, u32[]{:S(2)}, u32[]{:S(2)}) %all-to-all-start.2) | async-done | bytes 1048608 | tf_op jit(solution)/shard_map/all_to_all | solution.py:332
  96.7 0.0 copy-start.2
  96.7 1.0 copy-done.2
  97.7 3.1 %sum_step.1 = bf16[8,4,8,256]{3,2,1,0:T(8,128)(2,1)} custom-call(s32[130]{0:T(256)} %pad_add_fusion.1.meta, bf16[64,2,4,8,128]{4,3,2,1,0:T(8,128)(2,1)} %bitcast.89), custom_call_target="tpu_custom_call" | custom-call | tf_op jit(solution)/shard_map/sum_step/pallas_call | solution.py:276
  100.7 3.7 %all-to-all-start.3 = ((bf16[8,4,8,256]{3,2,1,0:T(8,128)(2,1)}), bf16[8,4,8,256]{3,2,1,0:T(8,128)(2,1)S(1)}, u32[]{:S(2)}, u32[]{:S(2)}) async-start(bf16[8,4,8,256]{3,2,1,0:T(8,128)(2,1)} %sum_step.1), calls=%async_computation.3 | async-start | bytes 262144 | tf_op jit(solution)/shard_map/all_to_all | solution.py:335
  104.4 1.9 %broadcast_select_fusion = f32[2]{0:T(128)} fusion(f32[2]{0:T(128)S(1)} %rev.3, pred[]{:T(512)S(6)} %eq.130, f32[1]{0:T(128)} %collective-permute-done.1, f32[1]{0:T(128)} %bitcast.43), kind=kLoop, calls=%fused_computation.84 | loop fusion | flops 4 | bytes 25 | tf_op jit(solution)/shard_map/jit(_where)/select_n | solution.py:343
  106.3 3.9 %all-to-all-done.3 = bf16[8,4,8,256]{3,2,1,0:T(8,128)(2,1)S(1)} async-done(((bf16[8,4,8,256]{3,2,1,0:T(8,128)(2,1)}), bf16[8,4,8,256]{3,2,1,0:T(8,128)(2,1)S(1)}, u32[]{:S(2)}, u32[]{:S(2)}) %all-to-all-start.3) | async-done | bytes 131104 | tf_op jit(solution)/shard_map/all_to_all | solution.py:335
  110.3 1.1 fusion.9
  (21 shorter events, 0.3 us)
Async XLA Ops:
  0.6 2.0 %copy-start = (bf16[2,2,512,32]{2,3,1,0:T(8,128)(2,1)S(1)}, bf16[2,2,512,32]{2,3,1,0:T(8,128)(2,1)}, u32[]{:S(2)}) copy-start(bf16[2,2,512,32]{2,3,1,0:T(8,128)(2,1)} %param.12) | copy-start | bytes 393220
  4.1 22.9 %all-to-all-start = ((bf16[128,8,128]{2,1,0:T(8,128)(2,1)}), bf16[128,8,128]{2,1,0:T(8,128)(2,1)S(1)}, u32[]{:S(2)}, u32[]{:S(2)}) async-start(bf16[128,8,128]{2,1,0:T(8,128)(2,1)} %copy.44), calls=%async_computation | async-start | bytes 524288 | tf_op jit(solution)/shard_map/all_to_all | solution.py:302
  52.7 2.7 %copy-start.1 = (bf16[128,4,8,128]{3,2,1,0:T(8,128)(2,1)}, bf16[128,4,8,128]{3,2,1,0:T(8,128)(2,1)S(1)}, u32[]{:S(2)}) copy-start(bf16[128,4,8,128]{3,2,1,0:T(8,128)(2,1)S(1)} %all_to_all.20) | copy-start | bytes 3145732
  52.7 2.7 %collective-permute-start = (bf16[32,2,2,4,8,128]{5,4,3,2,1,0:T(8,128)(2,1)S(1)}, bf16[32,2,2,4,8,128]{5,4,3,2,1,0:T(8,128)(2,1)S(1)}, u32[]{:S(2)}, u32[]{:S(2)}) collective-permute-start(bf16[32,2,2,4,8,128]{5,4,3,2,1,0:T(8,128)(2,1)S(1)} %bitcast.87), channel_id=1, source_target_pairs={{0,1},{1,0},{2,3},{3,2},{4,5},{5,4},{6,7},{7,6},{8,9},{9,8},{10,11... | collective-permute-start | bytes 3145736 | tf_op jit(solution)/shard_map/ppermute | solution.py:328
  55.4 1.0 copy-start.3
  73.4 23.3 %all-to-all-start.2 = ((bf16[128,4,8,128]{3,2,1,0:T(8,128)(2,1)}), bf16[128,4,8,128]{3,2,1,0:T(8,128)(2,1)S(1)}, u32[]{:S(2)}, u32[]{:S(2)}) async-start(bf16[128,4,8,128]{3,2,1,0:T(8,128)(2,1)} %bitcast.91), calls=%async_computation.2 | async-start | bytes 2097152 | tf_op jit(solution)/shard_map/all_to_all | solution.py:332
  79.2 7.0 %collective-permute-start.1 = (f32[1]{0:T(128)}, f32[1]{0:T(128)}, u32[]{:S(2)}, u32[]{:S(2)}) collective-permute-start(f32[1]{0:T(128)} %bitcast.43), channel_id=1, source_target_pairs={{0,2},{2,0},{1,3},{3,1},{4,6},{6,4},{5,7},{7,5},{8,10},{10,8},{9,1... | collective-permute-start | bytes 20 | tf_op jit(solution)/shard_map/ppermute | solution.py:341
  96.7 1.0 copy-start.2
  100.7 9.5 %all-to-all-start.3 = ((bf16[8,4,8,256]{3,2,1,0:T(8,128)(2,1)}), bf16[8,4,8,256]{3,2,1,0:T(8,128)(2,1)S(1)}, u32[]{:S(2)}, u32[]{:S(2)}) async-start(bf16[8,4,8,256]{3,2,1,0:T(8,128)(2,1)} %sum_step.1), calls=%async_computation.3 | async-start | bytes 262144 | tf_op jit(solution)/shard_map/all_to_all | solution.py:335

commit v2 on v1

--- a/solution.py
+++ b/solution.py
@@ -191,11 +191,15 @@
 PARAMS = pltpu.CompilerParams(vmem_limit_bytes=56 * 2**20)
 
 
+def placed(value):
+    return pltpu.with_memory_space_constraint(value, pltpu.VMEM)
+
+
 def probe_step(core, own, other, wave, measured, tables):
     return pl.pallas_call(
         probe_kernel,
         out_shape=(
-            jax.ShapeDtypeStruct((2, 16, 2, 2, 4, 8, 128), BF),
+            pltpu.VMEM((2, 16, 2, 2, 4, 8, 128), BF),
             jax.ShapeDtypeStruct((8, 128), F32),
         ),
         in_specs=[SM, VM, VM, VM] + [ANY] * 5,
@@ -212,16 +216,52 @@
         + [pltpu.SemaphoreType.DMA((5,))],
         compiler_params=PARAMS,
         name="probe_step",
-    )(core.reshape(1), own, other, wave, measured, *tables)
-
-
-def roll_kernel(meta, illumination, intensities, wave, measured, raw, sem):
-    copy = pltpu.make_async_copy(intensities.at[meta[2]], raw, sem)
-    copy.start()
+    )(core.reshape(1), placed(own), placed(other), placed(wave), measured, *tables)
+
+
+def corner(positions, owner, k):
+    return owner[k] * TILE_ROWS - BORDER + positions[k, 0], positions[k, 1]
+
+
+def prepare_kernel(positions, owner, block, out, rows):
     at0 = lax.broadcasted_iota(jnp.int32, (FRAME, FRAME), 0)
     at1 = lax.broadcasted_iota(jnp.int32, (FRAME, FRAME), 1)
-    cols = jnp.where(((natural(at0) - meta[1]) & (FRAME - 1)) == at1, 1.0, 0.0).astype(BF)
-    rows = jnp.where(((natural(at1) - meta[0]) & (FRAME - 1)) == at0, 1.0, 0.0).astype(BF)
+    place = jnp.where(natural(at1) == at0, 1.0, 0.0).astype(BF)
+    got = jnp.dot(block[...], place, preferred_element_type=F32)
+    lane = lax.broadcasted_iota(jnp.int32, (128, 128), 1)
+    info = jnp.zeros((128, 128), jnp.int32)
+    for k in range(2):
+        for n, value in enumerate(corner(positions, owner, k)):
+            info = jnp.where(lane == 4 * k + 2 * n, value >> 5, info)
+            info = jnp.where(lane == 4 * k + 2 * n + 1, value & 31, info)
+    for q in range(4):
+        rows[q, 0:128] = got[:, q * 128 : q * 128 + 128]
+        rows[q, 128:256] = info.astype(F32)
+    for i in range(32):
+        for q in range(4):
+            out[i, q % 2, q // 2] = rows[q, pl.ds(i, 8, stride=32), :].astype(BF)
+
+
+def prepare_step(positions, owner, block):
+    return pl.pallas_call(
+        prepare_kernel,
+        out_shape=pltpu.VMEM((32, 2, 2, 8, 128), BF),
+        in_specs=[SM, SM, VM],
+        out_specs=VM,
+        scratch_shapes=[pltpu.VMEM((4, 256, 128), F32)],
+        compiler_params=PARAMS,
+        name="prepare_step",
+    )(positions, owner, block)
+
+
+def roll_kernel(positions, owner, which, illumination, intensities, wave, measured, raw, sem):
+    copy = pltpu.make_async_copy(intensities.at[which[0]], raw, sem)
+    copy.start()
+    row0, col0 = corner(positions, owner, which[0])
+    at0 = lax.broadcasted_iota(jnp.int32, (FRAME, FRAME), 0)
+    at1 = lax.broadcasted_iota(jnp.int32, (FRAME, FRAME), 1)
+    cols = jnp.where(((natural(at0) - col0) & (FRAME - 1)) == at1, 1.0, 0.0).astype(BF)
+    rows = jnp.where(((natural(at1) - row0) & (FRAME - 1)) == at0, 1.0, 0.0).astype(BF)
     for part in range(2):
         turned = lax.dot_general(cols, illumination[part], (NT, ((), ())), preferred_element_type=F32)
         wave[part] = jnp.dot(turned.astype(BF), rows, preferred_element_type=F32).astype(BF)
@@ -229,19 +269,19 @@
     measured[...] = raw[...].T
 
 
-def roll_step(meta, illumination, intensities):
+def roll_step(positions, owner, which, illumination, intensities):
     return pl.pallas_call(
         roll_kernel,
         out_shape=(
-            jax.ShapeDtypeStruct((2, FRAME, FRAME), BF),
+            pltpu.VMEM((2, FRAME, FRAME), BF),
             jax.ShapeDtypeStruct((FRAME, FRAME), F32),
         ),
-        in_specs=[SM, VM, ANY],
+        in_specs=[SM, SM, SM, VM, ANY],
         out_specs=(VM, VM),
         scratch_shapes=[pltpu.VMEM((FRAME, FRAME), F32), pltpu.SemaphoreType.DMA],
         compiler_params=PARAMS,
         name="roll_step",
-    )(meta, illumination, intensities)
+    )(positions, owner, which.reshape(1), illumination, intensities)
 
 
 def sum_kernel(meta, parts, out, acc):
@@ -275,13 +315,13 @@
 def sum_step(meta, parts):
     return pl.pallas_call(
         sum_kernel,
-        out_shape=jax.ShapeDtypeStruct((8, 4, 8, 256), BF),
+        out_shape=pltpu.VMEM((8, 4, 8, 256), BF),
         in_specs=[SM, VM],
         out_specs=VM,
         scratch_shapes=[pltpu.VMEM((2, 5, 4, 2, 8, 128), F32)],
         compiler_params=PARAMS,
         name="sum_step",
-    )(meta, parts)
+    )(meta, placed(parts))
 
 
 def body(transmission, illumination, intensities, scan_positions, tile_owner):
@@ -292,17 +332,12 @@
     order = jnp.arange(FRAME, dtype=jnp.int32)
     residue = natural(order)
 
-    row0 = tile_owner * TILE_ROWS - BORDER + scan_positions[:, 0]
-    col0 = scan_positions[:, 1]
-    info = jnp.stack([row0 // 32, row0 % 32, col0 // 32, col0 % 32], axis=1).reshape(8).astype(BF)
     place = (residue[None, :] == order[:, None]).astype(BF)
-    block = dot(transmission.reshape(4, 512, 32), place, ((1,), (0,))).astype(BF)
-    block = block.reshape(4, 32, 2, 2, 128).transpose(1, 3, 2, 0, 4).reshape(128, 4, 128)
-    info = jnp.broadcast_to(jnp.pad(info, (0, 120)), (128, 4, 128))
-    got = lax.all_to_all(jnp.concatenate([block, info], axis=1), ALL, 0, 0, tiled=True)
-
-    mine = jnp.stack([row0, col0], axis=1)[which]
-    wave, measured = roll_step(jnp.concatenate([mine, which.reshape(1)]), illumination, intensities)
+    block = placed(transmission.transpose(0, 1, 3, 2).reshape(128, 512))
+    sent = prepare_step(scan_positions, tile_owner, block)
+    got = lax.all_to_all(sent.reshape(128, 8, 128), ALL, 0, 0, tiled=True)
+
+    wave, measured = roll_step(scan_positions, tile_owner, which, illumination, intensities)
     tables = (
         right_form(prop_re, prop_im),
         right_form(prop_re, -prop_im),

time: 112 us -> 107 us (0.955)
  local copies, waits for them, and re-layouts: 6.39 us -> 2.9 us
  other arithmetic: 7.29 us -> 5.91 us
    unnamed x9 -> x2, local copies, waits for them, and re-layouts: 2.04 us -> 0.9 us
    pallas_call x3 -> x4, Pallas kernels: 24.1 us -> 23.6 us  [the longest x1 15.2 us: probe_step(): pl.pallas_call(probe_kernel, out_shape=(pltpu.VMEM((2, 16, 2, 2, 4, 8, 12...]
where the time goes in v2:
time: 107 us; the launch traced here: 106 us
  waiting for transfers between devices  28 us (26%)
  Pallas kernels  23.6 us (22%)
  blocking collectives  23 us (21%)
  starting transfers between devices  21 us (20%)
  other arithmetic  5.91 us (6%)
  local copies, waits for them, and re-layouts  2.9 us (3%)
    all_to_all x1, blocking collectives, body(): lax.all_to_all(sent.reshape(128, 4, 8, 128), ALL, 0, 0, tiled=True)  23 us
    pallas_call x1, Pallas kernels, probe_step(): pl.pallas_call(probe_kernel, out_shape=(pltpu.VMEM((2, 16, 2, 2, 4, 8, 12...  15.2 us
    all_to_all x1, starting transfers between devices, body(): got = lax.all_to_all(sent.reshape(128, 8, 128), ALL, 0, 0, tiled=True)  11.5 us
    all_to_all x1, waiting for transfers between devices, body(): home = lax.all_to_all(grad.reshape(128, 4, 8, 128), ALL, 0, 0, tiled=True)  9.07 us
    all_to_all x1, waiting for transfers between devices, body(): got = lax.all_to_all(sent.reshape(128, 8, 128), ALL, 0, 0, tiled=True)  7.41 us
    ppermute x1, waiting for transfers between devices, body(): loss_other = lax.ppermute(loss, 'zl', [(0, 1), (1, 0)])  5.34 us
    all_to_all x1, waiting for transfers between devices, body(): final = lax.all_to_all(sums, SHARERS, 0, 0, tiled=True)  3.94 us
    pallas_call x1, Pallas kernels, roll_step(): pl.pallas_call(roll_kernel, out_shape=(pltpu.VMEM((2, FRAME, FRAME), BF),...  3.93 us
  transfers between devices with their start and end apart: 5, of which 5 were waited for; matrix products, arithmetic and copies ran while one was open for 5% of the time, Pallas kernels for 4%

profile of v2, /device:TPU:1, one launch (start us, length us, event | category | flops | bytes accessed | tf_op | source)
XLA Modules:
  0.0 106.4 jit_solution(13299584362218176588)
XLA Ops:
  0.6 0.0 copy-start
  0.6 0.9 copy-done
  1.5 1.9 %prepare_step.1 = bf16[32,2,2,8,128]{4,3,2,1,0:T(8,128)(2,1)} custom-call(s32[2,2]{1,0:T(2,128)} %positions.3, s32[2]{0:T(128)} %owner.3, bf16[128,512]{1,0:T(8,128)(2,1)S(1)} %bitcast.76), custom_call_target="tpu_custom_call" | custom-call | tf_op jit(solution)/shard_map/prepare_step/pallas_call | solution.py:246
  3.5 11.5 %all-to-all-start = ((bf16[128,8,128]{2,1,0:T(8,128)(2,1)}), bf16[128,8,128]{2,1,0:T(8,128)(2,1)S(1)}, u32[]{:S(2)}, u32[]{:S(2)}) async-start(bf16[128,8,128]{2,1,0:T(8,128)(2,1)} %bitcast.3), calls=%async_computation | async-start | bytes 524288 | tf_op jit(solution)/shard_map/all_to_all | solution.py:338
  15.0 3.9 %roll_step.1 = (bf16[2,512,512]{2,1,0:T(8,128)(2,1)S(1)}, f32[512,512]{1,0:T(8,128)}) custom-call(s32[2,2]{1,0:T(2,128)} %positions.3, s32[2]{0:T(128)} %owner.3, s32[1]{0:T(128)} %bitcast.4.which, bf16[2,512,512]{2,1,0:T(8,128)(2,1)} %illumination.1, f32[2,512,512]{2,1,0:T(8,128)} %intensities.1), custom_call_target="tpu_custom_call" | custom-call | tf_op jit(solution)/shard_map/roll_step/pallas_call | solution.py:273
  18.9 7.4 %all-to-all-done = bf16[128,8,128]{2,1,0:T(8,128)(2,1)S(1)} async-done(((bf16[128,8,128]{2,1,0:T(8,128)(2,1)}), bf16[128,8,128]{2,1,0:T(8,128)(2,1)S(1)}, u32[]{:S(2)}, u32[]{:S(2)}) %all-to-all-start) | async-done | bytes 262176 | tf_op jit(solution)/shard_map/all_to_all | solution.py:338
  26.4 0.1 convert_reduce_fusion
  26.5 0.1 reshape.253
  26.5 0.2 fusion.12
  26.8 0.1 lt.70
  26.9 0.1 lt.71
  27.0 0.2 fusion.28
  27.3 0.1 compare_select_fusion
  27.3 0.1 convert_add_fusion
  27.5 0.7 add_compare_fusion.7
  28.2 0.8 fusion.6
  29.0 23.0 %all_to_all.20 = bf16[128,4,8,128]{3,2,1,0:T(8,128)(2,1)S(1)} all-to-all(bf16[128,4,8,128]{3,2,1,0:T(8,128)(2,1)S(1)} %fusion.6), channel_id=1, replica_groups=mesh['half'=2,'col'=16,'zl'=2,'core'=2] {'half','col','zl','core'}, dimensions={0} | all-to-all | bytes 2097152 | tf_op jit(solution)/shard_map/all_to_all | solution.py:362
  52.1 0.4 collective-permute-start
  52.5 2.3 %collective-permute-done.other = bf16[32,2,2,4,8,128]{5,4,3,2,1,0:T(8,128)(2,1)S(1)} collective-permute-done((bf16[32,2,2,4,8,128]{5,4,3,2,1,0:T(8,128)(2,1)S(1)}, bf16[32,2,2,4,8,128]{5,4,3,2,1,0:T(8,128)(2,1)S(1)}, u32[]{:S(2)}, u32[]{:S(2)}) %collective-permute-start) | collective-permute-done | bytes 1048608 | tf_op jit(solution)/shard_map/ppermute | solution.py:363
  54.8 15.2 %probe_step.1 = (bf16[2,16,2,2,4,8,128]{6,5,4,3,2,1,0:T(8,128)(2,1)}, f32[8,128]{1,0:T(8,128)}) custom-call(s32[1]{0:T(128)} %bitcast.5.core_ref, bf16[32,2,2,4,8,128]{5,4,3,2,1,0:T(8,128)(2,1)S(1)} %bitcast.74, bf16[32,2,2,4,8,128]{5,4,3,2,1,0:T(8,128)(2,1)S(1)} %collective-permute-done.other, bf16[2,512,512]{2,1,0:T(8,128)(2,1)S(1)} %get-tuple-element.12.wave, ...), custom_call_target="tpu_custom_call" | custom-call | tf_op jit(solution)/shard_map/probe_step/pallas_call | solution.py:199
  70.0 3.8 %all-to-all-start.2 = ((bf16[128,4,8,128]{3,2,1,0:T(8,128)(2,1)}), bf16[128,4,8,128]{3,2,1,0:T(8,128)(2,1)S(1)}, u32[]{:S(2)}, u32[]{:S(2)}) async-start(bf16[128,4,8,128]{3,2,1,0:T(8,128)(2,1)} %bitcast.29), calls=%async_computation.2 | async-start | bytes 2097152 | tf_op jit(solution)/shard_map/all_to_all | solution.py:367
  73.9 0.7 pad_add_fusion.meta
  74.5 1.3 %slice.59 = f32[1,1]{1,0:T(1,128)} slice(f32[8,128]{1,0:T(8,128)} %get-tuple-element.15), slice={[0:1], [0:1]} | slice | bytes 8 | tf_op jit(solution)/shard_map/slice | solution.py:375
  75.8 1.6 %collective-permute-start.1 = (f32[1]{0:T(128)}, f32[1]{0:T(128)}, u32[]{:S(2)}, u32[]{:S(2)}) collective-permute-start(f32[1]{0:T(128)} %bitcast.36), channel_id=1, source_target_pairs={{0,2},{2,0},{1,3},{3,1},{4,6},{6,4},{5,7},{7,5},{8,10},{10,8},{9,1... | collective-permute-start | bytes 20 | tf_op jit(solution)/shard_map/ppermute | solution.py:376
  77.4 5.3 %collective-permute-done.1 = f32[1]{0:T(128)} collective-permute-done((f32[1]{0:T(128)}, f32[1]{0:T(128)}, u32[]{:S(2)}, u32[]{:S(2)}) %collective-permute-start.1) | collective-permute-done | bytes 36 | tf_op jit(solution)/shard_map/ppermute | solution.py:376
  82.7 1.4 %pad_maximum_fusion = f32[2]{0:T(128)S(1)} fusion(f32[1]{0:T(128)} %collective-permute-done.1, f32[1]{0:T(128)} %bitcast.36), kind=kLoop, calls=%fused_computation.69 | loop fusion | flops 2 | bytes 16 | tf_op jit(solution)/shard_map/concatenate | solution.py:377
  84.1 0.1 rev.3
  84.2 9.1 %all-to-all-done.2 = bf16[128,4,8,128]{3,2,1,0:T(8,128)(2,1)S(1)} async-done(((bf16[128,4,8,128]{3,2,1,0:T(8,128)(2,1)}), bf16[128,4,8,128]{3,2,1,0:T(8,128)(2,1)S(1)}, u32[]{:S(2)}, u32[]{:S(2)}) %all-to-all-start.2) | async-done | bytes 1048608 | tf_op jit(solution)/shard_map/all_to_all | solution.py:367
  93.3 2.5 %sum_step.1 = bf16[8,4,8,256]{3,2,1,0:T(8,128)(2,1)} custom-call(s32[130]{0:T(256)} %pad_add_fusion.meta, bf16[64,2,4,8,128]{4,3,2,1,0:T(8,128)(2,1)S(1)} %bitcast.75), custom_call_target="tpu_custom_call" | custom-call | tf_op jit(solution)/shard_map/sum_step/pallas_call | solution.py:316
  95.8 3.7 %all-to-all-start.3 = ((bf16[8,4,8,256]{3,2,1,0:T(8,128)(2,1)}), bf16[8,4,8,256]{3,2,1,0:T(8,128)(2,1)S(1)}, u32[]{:S(2)}, u32[]{:S(2)}) async-start(bf16[8,4,8,256]{3,2,1,0:T(8,128)(2,1)} %sum_step.1), calls=%async_computation.3 | async-start | bytes 262144 | tf_op jit(solution)/shard_map/all_to_all | solution.py:370
  99.5 1.9 %broadcast_select_fusion = f32[2]{0:T(128)} fusion(f32[2]{0:T(128)S(1)} %rev.3, pred[]{:T(512)S(6)} %eq.121, f32[1]{0:T(128)} %collective-permute-done.1, f32[1]{0:T(128)} %bitcast.36), kind=kLoop, calls=%fused_computation.66 | loop fusion | flops 4 | bytes 25 | tf_op jit(solution)/shard_map/jit(_where)/select_n | solution.py:378
  101.4 3.9 %all-to-all-done.3 = bf16[8,4,8,256]{3,2,1,0:T(8,128)(2,1)S(1)} async-done(((bf16[8,4,8,256]{3,2,1,0:T(8,128)(2,1)}), bf16[8,4,8,256]{3,2,1,0:T(8,128)(2,1)S(1)}, u32[]{:S(2)}, u32[]{:S(2)}) %all-to-all-start.3) | async-done | bytes 131104 | tf_op jit(solution)/shard_map/all_to_all | solution.py:370
  105.3 1.1 fusion.8
  (12 shorter events, 0.2 us)
Async XLA Ops:
  0.6 0.9 copy-start
  3.5 22.9 %all-to-all-start = ((bf16[128,8,128]{2,1,0:T(8,128)(2,1)}), bf16[128,8,128]{2,1,0:T(8,128)(2,1)S(1)}, u32[]{:S(2)}, u32[]{:S(2)}) async-start(bf16[128,8,128]{2,1,0:T(8,128)(2,1)} %bitcast.3), calls=%async_computation | async-start | bytes 524288 | tf_op jit(solution)/shard_map/all_to_all | solution.py:338
  52.1 2.7 %collective-permute-start = (bf16[32,2,2,4,8,128]{5,4,3,2,1,0:T(8,128)(2,1)S(1)}, bf16[32,2,2,4,8,128]{5,4,3,2,1,0:T(8,128)(2,1)S(1)}, u32[]{:S(2)}, u32[]{:S(2)}) collective-permute-start(bf16[32,2,2,4,8,128]{5,4,3,2,1,0:T(8,128)(2,1)S(1)} %bitcast.73), channel_id=1, source_target_pairs={{0,1},{1,0},{2,3},{3,2},{4,5},{5,4},{6,7},{7,6},{8,9},{9,8},{10,11... | collective-permute-start | bytes 3145736 | tf_op jit(solution)/shard_map/ppermute | solution.py:363
  70.0 23.3 %all-to-all-start.2 = ((bf16[128,4,8,128]{3,2,1,0:T(8,128)(2,1)}), bf16[128,4,8,128]{3,2,1,0:T(8,128)(2,1)S(1)}, u32[]{:S(2)}, u32[]{:S(2)}) async-start(bf16[128,4,8,128]{3,2,1,0:T(8,128)(2,1)} %bitcast.29), calls=%async_computation.2 | async-start | bytes 2097152 | tf_op jit(solution)/shard_map/all_to_all | solution.py:367
  75.8 7.0 %collective-permute-start.1 = (f32[1]{0:T(128)}, f32[1]{0:T(128)}, u32[]{:S(2)}, u32[]{:S(2)}) collective-permute-start(f32[1]{0:T(128)} %bitcast.36), channel_id=1, source_target_pairs={{0,2},{2,0},{1,3},{3,1},{4,6},{6,4},{5,7},{7,5},{8,10},{10,8},{9,1... | collective-permute-start | bytes 20 | tf_op jit(solution)/shard_map/ppermute | solution.py:376
  95.8 9.5 %all-to-all-start.3 = ((bf16[8,4,8,256]{3,2,1,0:T(8,128)(2,1)}), bf16[8,4,8,256]{3,2,1,0:T(8,128)(2,1)S(1)}, u32[]{:S(2)}, u32[]{:S(2)}) async-start(bf16[8,4,8,256]{3,2,1,0:T(8,128)(2,1)} %sum_step.1), calls=%async_computation.3 | async-start | bytes 262144 | tf_op jit(solution)/shard_map/all_to_all | solution.py:370

commit v3 on v2

--- a/solution.py
+++ b/solution.py
@@ -58,17 +58,16 @@
 
 
 def probe_kernel(
-    core_ref, own, other, wave, measured_hbm, bq_hbm, aq_hbm, bw_hbm, aw_hbm, out, loss,
-    y, inner, x1, field, turn, measured, bq, aq, bw, aw, sems,
+    core_ref, own, other, wave, bq, measured_hbm, aq_hbm, bw_hbm, aw_hbm, out, loss,
+    y, inner, x1, field, turn, measured, aq, bw, aw, sems,
 ):
     copies = [
         pltpu.make_async_copy(src, dst, sems.at[n])
         for n, (src, dst) in enumerate(
-            ((bq_hbm, bq), (aq_hbm, aq), (bw_hbm, bw), (aw_hbm, aw), (measured_hbm, measured))
+            ((aq_hbm, aq), (bw_hbm, bw), (aw_hbm, aw), (measured_hbm, measured))
         )
     ]
-    for copy in copies:
-        copy.start()
+    copies[0].start()
     core = core_ref[0]
     first = core == 0
     here = pl.multiple_of(core * 256, 256)
@@ -115,10 +114,9 @@
             inner[n // 2 * 512 : n // 2 * 512 + 512, n % 2 * 256 : n % 2 * 256 + 256] = got.astype(BF)
 
     def left(table, dst):
-        for n in range(2):
-            dst[:, n * 256 : n * 256 + 256] = jnp.dot(
-                table[...], inner[:, n * 256 : n * 256 + 256], preferred_element_type=F32
-            )
+        for n in range(4):
+            rows = slice(n * 256, n * 256 + 256)
+            dst[rows, :] = jnp.dot(table[rows, :], inner[...], preferred_element_type=F32)
 
     def hand_out(plane):
         for o in range(4):
@@ -129,16 +127,17 @@
                         out[o // 2, j, o % 2, z, plane + part] = turn[z, rows, :].astype(BF)
 
     product(0, from_wave, False)
+    right(bq)
     copies[0].wait()
-    right(bq)
-    copies[1].wait()
+    for copy in copies[1:]:
+        copy.start()
     left(aq, x1)
     product(2, from_ref(x1), False)
+    copies[1].wait()
+    right(bw)
     copies[2].wait()
-    right(bw)
+    left(aw, field)
     copies[3].wait()
-    left(aw, field)
-    copies[4].wait()
 
     def compare(i, total):
         rows, rows_im = block_rows(i)
@@ -170,7 +169,9 @@
         cols = pl.ds(pl.multiple_of(here + part * 512, 256), 256)
         got = jnp.dot(y[...], aq[:, cols], preferred_element_type=F32)
         inner[part * 512 : part * 512 + 512, 0:256] = got.astype(BF)
-    field[:, 0:256] = jnp.dot(bq[...], inner[:, 0:256], preferred_element_type=F32)
+    for n in range(4):
+        rows = slice(n * 256, n * 256 + 256)
+        field[rows, 0:256] = jnp.dot(bq[rows, :], inner[:, 0:256], preferred_element_type=F32)
 
     def gradient0(i, _):
         rows, rows_im = block_rows(i)
@@ -202,7 +203,7 @@
             pltpu.VMEM((2, 16, 2, 2, 4, 8, 128), BF),
             jax.ShapeDtypeStruct((8, 128), F32),
         ),
-        in_specs=[SM, VM, VM, VM] + [ANY] * 5,
+        in_specs=[SM] + [VM] * 4 + [ANY] * 4,
         out_specs=(VM, VM),
         scratch_shapes=[
             pltpu.VMEM((512, 1024), BF),
@@ -212,11 +213,11 @@
             pltpu.VMEM((2, 1024, 128), F32),
             pltpu.VMEM((512, 512), F32),
         ]
-        + [pltpu.VMEM((1024, 1024), BF)] * 4
-        + [pltpu.SemaphoreType.DMA((5,))],
+        + [pltpu.VMEM((1024, 1024), BF)] * 3
+        + [pltpu.SemaphoreType.DMA((4,))],
         compiler_params=PARAMS,
         name="probe_step",
-    )(core.reshape(1), placed(own), placed(other), placed(wave), measured, *tables)
+    )(core.reshape(1), placed(own), placed(other), placed(wave), placed(tables[0]), measured, *tables[1:])
 
 
 def corner(positions, owner, k):
@@ -304,7 +305,7 @@
                     acc[1, tile, plane, c] += jnp.where(right, piece, 0.0)
         return 0
 
-    lax.fori_loop(0, 64, step, 0)
+    lax.fori_loop(0, 64, step, 0, unroll=4)
     for h in range(2):
         for tile in range(4):
             for plane in range(4):

time: 107 us -> 105 us (0.981)
  Pallas kernels: 23.6 us -> 21.4 us
    pallas_call x1, Pallas kernels: 15.2 us -> 13.2 us  [probe_step(): pl.pallas_call(probe_kernel, out_shape=(pltpu.VMEM((2, 16, 2, 2, 4, 8, 12...]
where the time goes in v3:
time: 105 us; the launch traced here: 104 us
  waiting for transfers between devices  27.2 us (26%)
  blocking collectives  23 us (22%)
  Pallas kernels  21.4 us (20%)
  starting transfers between devices  21 us (20%)
  other arithmetic  5.78 us (6%)
  local copies, waits for them, and re-layouts  3.87 us (4%)
  matrix products  1.05 us (1%)
    all_to_all x1, blocking collectives, body(): lax.all_to_all(sent.reshape(128, 4, 8, 128), ALL, 0, 0, tiled=True)  23 us
    pallas_call x1, Pallas kernels, probe_step(): pl.pallas_call(probe_kernel, out_shape=(pltpu.VMEM((2, 16, 2, 2, 4, 8, 12...  13.2 us
    all_to_all x1, starting transfers between devices, body(): got = lax.all_to_all(sent.reshape(128, 8, 128), ALL, 0, 0, tiled=True)  11.5 us
    all_to_all x1, waiting for transfers between devices, body(): home = lax.all_to_all(grad.reshape(128, 4, 8, 128), ALL, 0, 0, tiled=True)  9.13 us
    all_to_all x1, waiting for transfers between devices, body(): got = lax.all_to_all(sent.reshape(128, 8, 128), ALL, 0, 0, tiled=True)  6.42 us
    ppermute x1, waiting for transfers between devices, body(): loss_other = lax.ppermute(loss, 'zl', [(0, 1), (1, 0)])  5.34 us
    all_to_all x1, waiting for transfers between devices, body(): final = lax.all_to_all(sums, SHARERS, 0, 0, tiled=True)  4.01 us
    pallas_call x1, Pallas kernels, roll_step(): pl.pallas_call(roll_kernel, out_shape=(pltpu.VMEM((2, FRAME, FRAME), BF),...  3.95 us
  transfers between devices with their start and end apart: 5, of which 5 were waited for; matrix products, arithmetic and copies ran while one was open for 5% of the time, Pallas kernels for 4%

profile of v3, /device:TPU:1, one launch (start us, length us, event | category | flops | bytes accessed | tf_op | source)
XLA Modules:
  0.0 104.2 jit_solution(5037547088733371298)
XLA Ops:
  0.6 0.0 copy-start.3
  0.6 0.9 copy-done.3
  1.5 1.9 %prepare_step.1 = bf16[32,2,2,8,128]{4,3,2,1,0:T(8,128)(2,1)} custom-call(s32[2,2]{1,0:T(2,128)} %positions.3, s32[2]{0:T(128)} %owner.3, bf16[128,512]{1,0:T(8,128)(2,1)S(1)} %bitcast.76), custom_call_target="tpu_custom_call" | custom-call | tf_op jit(solution)/shard_map/prepare_step/pallas_call | solution.py:247
  3.5 11.5 %all-to-all-start = ((bf16[128,8,128]{2,1,0:T(8,128)(2,1)}), bf16[128,8,128]{2,1,0:T(8,128)(2,1)S(1)}, u32[]{:S(2)}, u32[]{:S(2)}) async-start(bf16[128,8,128]{2,1,0:T(8,128)(2,1)} %bitcast.3), calls=%async_computation | async-start | bytes 524288 | tf_op jit(solution)/shard_map/all_to_all | solution.py:339
  15.0 4.0 %roll_step.1 = (bf16[2,512,512]{2,1,0:T(8,128)(2,1)S(1)}, f32[512,512]{1,0:T(8,128)}) custom-call(s32[2,2]{1,0:T(2,128)} %positions.3, s32[2]{0:T(128)} %owner.3, s32[1]{0:T(128)} %bitcast.4.which, bf16[2,512,512]{2,1,0:T(8,128)(2,1)} %illumination.1, f32[2,512,512]{2,1,0:T(8,128)} %intensities.1), custom_call_target="tpu_custom_call" | custom-call | tf_op jit(solution)/shard_map/roll_step/pallas_call | solution.py:274
  18.9 0.0 copy-start.1
  18.9 1.0 copy-done.1
  19.9 6.4 %all-to-all-done = bf16[128,8,128]{2,1,0:T(8,128)(2,1)S(1)} async-done(((bf16[128,8,128]{2,1,0:T(8,128)(2,1)}), bf16[128,8,128]{2,1,0:T(8,128)(2,1)S(1)}, u32[]{:S(2)}, u32[]{:S(2)}) %all-to-all-start) | async-done | bytes 262176 | tf_op jit(solution)/shard_map/all_to_all | solution.py:339
  26.4 0.1 convert_reduce_fusion
  26.5 0.1 reshape.253
  26.5 0.2 fusion.12
  26.8 0.1 lt.70
  26.9 0.1 lt.71
  27.0 0.2 fusion.28
  27.3 0.1 compare_select_fusion
  27.3 0.1 convert_add_fusion
  27.5 0.7 add_compare_fusion.7
  28.2 0.0 copy-start
  28.2 0.0 copy-start.2
  28.2 0.8 fusion.6
  29.1 23.0 %all_to_all.20 = bf16[128,4,8,128]{3,2,1,0:T(8,128)(2,1)S(1)} all-to-all(bf16[128,4,8,128]{3,2,1,0:T(8,128)(2,1)S(1)} %fusion.6), channel_id=1, replica_groups=mesh['half'=2,'col'=16,'zl'=2,'core'=2] {'half','col','zl','core'}, dimensions={0} | all-to-all | bytes 2097152 | tf_op jit(solution)/shard_map/all_to_all | solution.py:363
  52.1 0.4 collective-permute-start
  52.5 2.3 %collective-permute-done.other = bf16[32,2,2,4,8,128]{5,4,3,2,1,0:T(8,128)(2,1)S(1)} collective-permute-done((bf16[32,2,2,4,8,128]{5,4,3,2,1,0:T(8,128)(2,1)S(1)}, bf16[32,2,2,4,8,128]{5,4,3,2,1,0:T(8,128)(2,1)S(1)}, u32[]{:S(2)}, u32[]{:S(2)}) %collective-permute-start) | collective-permute-done | bytes 1048608 | tf_op jit(solution)/shard_map/ppermute | solution.py:364
  54.8 0.0 copy-done
  54.8 0.0 copy-done.2
  54.8 13.2 %probe_step.1 = (bf16[2,16,2,2,4,8,128]{6,5,4,3,2,1,0:T(8,128)(2,1)}, f32[8,128]{1,0:T(8,128)}) custom-call(s32[1]{0:T(128)} %bitcast.5.core_ref, bf16[32,2,2,4,8,128]{5,4,3,2,1,0:T(8,128)(2,1)S(1)} %bitcast.74, bf16[32,2,2,4,8,128]{5,4,3,2,1,0:T(8,128)(2,1)S(1)} %collective-permute-done.other, bf16[2,512,512]{2,1,0:T(8,128)(2,1)S(1)} %copy-done.2, ...), custom_call_target="tpu_custom_call" | custom-call | tf_op jit(solution)/shard_map/probe_step/pallas_call | solution.py:200
  68.0 3.8 %all-to-all-start.2 = ((bf16[128,4,8,128]{3,2,1,0:T(8,128)(2,1)}), bf16[128,4,8,128]{3,2,1,0:T(8,128)(2,1)S(1)}, u32[]{:S(2)}, u32[]{:S(2)}) async-start(bf16[128,4,8,128]{3,2,1,0:T(8,128)(2,1)} %bitcast.29), calls=%async_computation.2 | async-start | bytes 2097152 | tf_op jit(solution)/shard_map/all_to_all | solution.py:368
  71.8 0.7 pad_add_fusion.meta
  72.5 1.3 %slice.59 = f32[1,1]{1,0:T(1,128)} slice(f32[8,128]{1,0:T(8,128)} %get-tuple-element.15), slice={[0:1], [0:1]} | slice | bytes 8 | tf_op jit(solution)/shard_map/slice | solution.py:376
  73.8 1.6 %collective-permute-start.1 = (f32[1]{0:T(128)}, f32[1]{0:T(128)}, u32[]{:S(2)}, u32[]{:S(2)}) collective-permute-start(f32[1]{0:T(128)} %bitcast.36), channel_id=1, source_target_pairs={{0,2},{2,0},{1,3},{3,1},{4,6},{6,4},{5,7},{7,5},{8,10},{10,8},{9,1... | collective-permute-start | bytes 20 | tf_op jit(solution)/shard_map/ppermute | solution.py:377
  75.4 5.3 %collective-permute-done.1 = f32[1]{0:T(128)} collective-permute-done((f32[1]{0:T(128)}, f32[1]{0:T(128)}, u32[]{:S(2)}, u32[]{:S(2)}) %collective-permute-start.1) | collective-permute-done | bytes 36 | tf_op jit(solution)/shard_map/ppermute | solution.py:377
  80.7 1.3 %pad_maximum_fusion = f32[2]{0:T(128)S(1)} fusion(f32[1]{0:T(128)} %collective-permute-done.1, f32[1]{0:T(128)} %bitcast.36), kind=kLoop, calls=%fused_computation.69 | loop fusion | flops 2 | bytes 16 | tf_op jit(solution)/shard_map/concatenate | solution.py:378
  82.0 0.1 rev.3
  82.1 9.1 %all-to-all-done.2 = bf16[128,4,8,128]{3,2,1,0:T(8,128)(2,1)S(1)} async-done(((bf16[128,4,8,128]{3,2,1,0:T(8,128)(2,1)}), bf16[128,4,8,128]{3,2,1,0:T(8,128)(2,1)S(1)}, u32[]{:S(2)}, u32[]{:S(2)}) %all-to-all-start.2) | async-done | bytes 1048608 | tf_op jit(solution)/shard_map/all_to_all | solution.py:368
  91.3 2.3 %sum_step.1 = bf16[8,4,8,256]{3,2,1,0:T(8,128)(2,1)} custom-call(s32[130]{0:T(256)} %pad_add_fusion.meta, bf16[64,2,4,8,128]{4,3,2,1,0:T(8,128)(2,1)S(1)} %bitcast.75), custom_call_target="tpu_custom_call" | custom-call | tf_op jit(solution)/shard_map/sum_step/pallas_call | solution.py:317
  93.6 3.7 %all-to-all-start.3 = ((bf16[8,4,8,256]{3,2,1,0:T(8,128)(2,1)}), bf16[8,4,8,256]{3,2,1,0:T(8,128)(2,1)S(1)}, u32[]{:S(2)}, u32[]{:S(2)}) async-start(bf16[8,4,8,256]{3,2,1,0:T(8,128)(2,1)} %sum_step.1), calls=%async_computation.3 | async-start | bytes 262144 | tf_op jit(solution)/shard_map/all_to_all | solution.py:371
  97.3 1.8 %broadcast_select_fusion = f32[2]{0:T(128)} fusion(f32[2]{0:T(128)S(1)} %rev.3, pred[]{:T(512)S(6)} %eq.121, f32[1]{0:T(128)} %collective-permute-done.1, f32[1]{0:T(128)} %bitcast.36), kind=kLoop, calls=%fused_computation.66 | loop fusion | flops 4 | bytes 25 | tf_op jit(solution)/shard_map/jit(_where)/select_n | solution.py:379
  99.1 4.0 %all-to-all-done.3 = bf16[8,4,8,256]{3,2,1,0:T(8,128)(2,1)S(1)} async-done(((bf16[8,4,8,256]{3,2,1,0:T(8,128)(2,1)}), bf16[8,4,8,256]{3,2,1,0:T(8,128)(2,1)S(1)}, u32[]{:S(2)}, u32[]{:S(2)}) %all-to-all-start.3) | async-done | bytes 131104 | tf_op jit(solution)/shard_map/all_to_all | solution.py:371
  103.1 1.1 %fusion.8 = f32[512,4,32]{0,2,1:T(8,128)} fusion(bf16[4,32,512]{2,1,0:T(8,128)(2,1)S(1)} %bitcast.81, s32[512]{0:T(512)S(1)} %fusion.20), kind=kOutput, calls=%fused_computation.18 | convolution fusion | flops 67371008 | bytes 395264 | tf_op jit(solution)/shard_map/dot_general | solution.py:373
  (12 shorter events, 0.2 us)
Async XLA Ops:
  0.6 0.9 copy-start.3
  3.5 22.9 %all-to-all-start = ((bf16[128,8,128]{2,1,0:T(8,128)(2,1)}), bf16[128,8,128]{2,1,0:T(8,128)(2,1)S(1)}, u32[]{:S(2)}, u32[]{:S(2)}) async-start(bf16[128,8,128]{2,1,0:T(8,128)(2,1)} %bitcast.3), calls=%async_computation | async-start | bytes 524288 | tf_op jit(solution)/shard_map/all_to_all | solution.py:339
  18.9 1.0 copy-start.1
  28.2 26.6 %copy-start = (bf16[1024,1024]{1,0:T(8,128)(2,1)S(1)}, bf16[1024,1024]{1,0:T(8,128)(2,1)}, u32[]{:S(2)}) copy-start(bf16[1024,1024]{1,0:T(8,128)(2,1)} %constant.146.bq) | copy-start | bytes 6291460
  28.2 26.6 %copy-start.2 = (bf16[2,512,512]{2,1,0:T(8,128)(2,1)S(1)}, bf16[2,512,512]{2,1,0:T(8,128)(2,1)}, u32[]{:S(2)}) copy-start(bf16[2,512,512]{2,1,0:T(8,128)(2,1)} %copy-done.1) | copy-start | bytes 3145732
  52.1 2.7 %collective-permute-start = (bf16[32,2,2,4,8,128]{5,4,3,2,1,0:T(8,128)(2,1)S(1)}, bf16[32,2,2,4,8,128]{5,4,3,2,1,0:T(8,128)(2,1)S(1)}, u32[]{:S(2)}, u32[]{:S(2)}) collective-permute-start(bf16[32,2,2,4,8,128]{5,4,3,2,1,0:T(8,128)(2,1)S(1)} %bitcast.73), channel_id=1, source_target_pairs={{0,1},{1,0},{2,3},{3,2},{4,5},{5,4},{6,7},{7,6},{8,9},{9,8},{10,11... | collective-permute-start | bytes 3145736 | tf_op jit(solution)/shard_map/ppermute | solution.py:364
  68.0 23.3 %all-to-all-start.2 = ((bf16[128,4,8,128]{3,2,1,0:T(8,128)(2,1)}), bf16[128,4,8,128]{3,2,1,0:T(8,128)(2,1)S(1)}, u32[]{:S(2)}, u32[]{:S(2)}) async-start(bf16[128,4,8,128]{3,2,1,0:T(8,128)(2,1)} %bitcast.29), calls=%async_computation.2 | async-start | bytes 2097152 | tf_op jit(solution)/shard_map/all_to_all | solution.py:368
  73.8 7.0 %collective-permute-start.1 = (f32[1]{0:T(128)}, f32[1]{0:T(128)}, u32[]{:S(2)}, u32[]{:S(2)}) collective-permute-start(f32[1]{0:T(128)} %bitcast.36), channel_id=1, source_target_pairs={{0,2},{2,0},{1,3},{3,1},{4,6},{6,4},{5,7},{7,5},{8,10},{10,8},{9,1... | collective-permute-start | bytes 20 | tf_op jit(solution)/shard_map/ppermute | solution.py:377
  93.6 9.5 %all-to-all-start.3 = ((bf16[8,4,8,256]{3,2,1,0:T(8,128)(2,1)}), bf16[8,4,8,256]{3,2,1,0:T(8,128)(2,1)S(1)}, u32[]{:S(2)}, u32[]{:S(2)}) async-start(bf16[8,4,8,256]{3,2,1,0:T(8,128)(2,1)} %sum_step.1), calls=%async_computation.3 | async-start | bytes 262144 | tf_op jit(solution)/shard_map/all_to_all | solution.py:371

commit v4 on v3

--- a/solution.py
+++ b/solution.py
@@ -80,7 +80,7 @@
         return pl.ds(pl.multiple_of(i * 16, 16), 16), pl.ds(pl.multiple_of(512 + i * 16, 16), 16)
 
     def product(plane, get, conj):
-        def step(i, _):
+        def step(i):
             rows, _ = block_rows(i)
             for z in range(2):
                 for c in range(2):
@@ -95,7 +95,8 @@
                     y[rows, 512 + at : 640 + at] = im.astype(BF)
             return 0
 
-        lax.fori_loop(0, 32, step, 0, unroll=2)
+        for i in range(32):
+            step(i)
 
     def from_wave(i, lanes):
         rows, _ = block_rows(i)

time: 105 us -> 104 us (level)
  no operation moved by 1% of the time
where the time goes in v4:
time: 104 us
  waiting for transfers between devices  27.2 us (26%)
  blocking collectives  23 us (22%)
  starting transfers between devices  21 us (20%)
  Pallas kernels  20.8 us (20%)
  other arithmetic  5.78 us (6%)
  local copies, waits for them, and re-layouts  3.87 us (4%)
  matrix products  1.05 us (1%)
    all_to_all x1, blocking collectives, body(): lax.all_to_all(sent.reshape(128, 4, 8, 128), ALL, 0, 0, tiled=True)  23 us
    pallas_call x1, Pallas kernels, probe_step(): pl.pallas_call(probe_kernel, out_shape=(pltpu.VMEM((2, 16, 2, 2, 4, 8, 12...  12.6 us
    all_to_all x1, starting transfers between devices, body(): got = lax.all_to_all(sent.reshape(128, 8, 128), ALL, 0, 0, tiled=True)  11.5 us
    all_to_all x1, waiting for transfers between devices, body(): home = lax.all_to_all(grad.reshape(128, 4, 8, 128), ALL, 0, 0, tiled=True)  9.13 us
    all_to_all x1, waiting for transfers between devices, body(): got = lax.all_to_all(sent.reshape(128, 8, 128), ALL, 0, 0, tiled=True)  6.42 us
    ppermute x1, waiting for transfers between devices, body(): loss_other = lax.ppermute(loss, 'zl', [(0, 1), (1, 0)])  5.34 us
    all_to_all x1, waiting for transfers between devices, body(): final = lax.all_to_all(sums, SHARERS, 0, 0, tiled=True)  4.01 us
    pallas_call x1, Pallas kernels, roll_step(): pl.pallas_call(roll_kernel, out_shape=(pltpu.VMEM((2, FRAME, FRAME), BF),...  3.95 us
  transfers between devices with their start and end apart: 5, of which 5 were waited for; matrix products, arithmetic and copies ran while one was open for 5% of the time, Pallas kernels for 4%

profile of v4, /device:TPU:1, one launch (start us, length us, event | category | flops | bytes accessed | tf_op | source)
XLA Modules:
  0.0 103.6 jit_solution(11280556239522589657)
XLA Ops:
  0.6 0.0 copy-start.3
  0.6 0.9 copy-done.3
  1.5 1.9 %prepare_step.1 = bf16[32,2,2,8,128]{4,3,2,1,0:T(8,128)(2,1)} custom-call(s32[2,2]{1,0:T(2,128)} %positions.3, s32[2]{0:T(128)} %owner.3, bf16[128,512]{1,0:T(8,128)(2,1)S(1)} %bitcast.76), custom_call_target="tpu_custom_call" | custom-call | tf_op jit(solution)/shard_map/prepare_step/pallas_call | solution.py:248
  3.5 11.5 %all-to-all-start = ((bf16[128,8,128]{2,1,0:T(8,128)(2,1)}), bf16[128,8,128]{2,1,0:T(8,128)(2,1)S(1)}, u32[]{:S(2)}, u32[]{:S(2)}) async-start(bf16[128,8,128]{2,1,0:T(8,128)(2,1)} %bitcast.3), calls=%async_computation | async-start | bytes 524288 | tf_op jit(solution)/shard_map/all_to_all | solution.py:340
  15.0 4.0 %roll_step.1 = (bf16[2,512,512]{2,1,0:T(8,128)(2,1)S(1)}, f32[512,512]{1,0:T(8,128)}) custom-call(s32[2,2]{1,0:T(2,128)} %positions.3, s32[2]{0:T(128)} %owner.3, s32[1]{0:T(128)} %bitcast.4.which, bf16[2,512,512]{2,1,0:T(8,128)(2,1)} %illumination.1, f32[2,512,512]{2,1,0:T(8,128)} %intensities.1), custom_call_target="tpu_custom_call" | custom-call | tf_op jit(solution)/shard_map/roll_step/pallas_call | solution.py:275
  18.9 0.0 copy-start.1
  18.9 1.0 copy-done.1
  19.9 6.4 %all-to-all-done = bf16[128,8,128]{2,1,0:T(8,128)(2,1)S(1)} async-done(((bf16[128,8,128]{2,1,0:T(8,128)(2,1)}), bf16[128,8,128]{2,1,0:T(8,128)(2,1)S(1)}, u32[]{:S(2)}, u32[]{:S(2)}) %all-to-all-start) | async-done | bytes 262176 | tf_op jit(solution)/shard_map/all_to_all | solution.py:340
  26.4 0.1 convert_reduce_fusion
  26.5 0.1 reshape.253
  26.5 0.2 fusion.12
  26.8 0.1 lt.70
  26.9 0.1 lt.71
  27.0 0.2 fusion.28
  27.3 0.1 compare_select_fusion
  27.3 0.1 convert_add_fusion
  27.5 0.7 add_compare_fusion.7
  28.2 0.0 copy-start
  28.2 0.0 copy-start.2
  28.2 0.8 fusion.6
  29.1 23.0 %all_to_all.20 = bf16[128,4,8,128]{3,2,1,0:T(8,128)(2,1)S(1)} all-to-all(bf16[128,4,8,128]{3,2,1,0:T(8,128)(2,1)S(1)} %fusion.6), channel_id=1, replica_groups=mesh['half'=2,'col'=16,'zl'=2,'core'=2] {'half','col','zl','core'}, dimensions={0} | all-to-all | bytes 2097152 | tf_op jit(solution)/shard_map/all_to_all | solution.py:364
  52.1 0.4 collective-permute-start
  52.5 2.3 %collective-permute-done.other = bf16[32,2,2,4,8,128]{5,4,3,2,1,0:T(8,128)(2,1)S(1)} collective-permute-done((bf16[32,2,2,4,8,128]{5,4,3,2,1,0:T(8,128)(2,1)S(1)}, bf16[32,2,2,4,8,128]{5,4,3,2,1,0:T(8,128)(2,1)S(1)}, u32[]{:S(2)}, u32[]{:S(2)}) %collective-permute-start) | collective-permute-done | bytes 1048608 | tf_op jit(solution)/shard_map/ppermute | solution.py:365
  54.8 0.0 copy-done
  54.8 0.0 copy-done.2
  54.8 12.6 %probe_step.1 = (bf16[2,16,2,2,4,8,128]{6,5,4,3,2,1,0:T(8,128)(2,1)}, f32[8,128]{1,0:T(8,128)}) custom-call(s32[1]{0:T(128)} %bitcast.5.core_ref, bf16[32,2,2,4,8,128]{5,4,3,2,1,0:T(8,128)(2,1)S(1)} %bitcast.74, bf16[32,2,2,4,8,128]{5,4,3,2,1,0:T(8,128)(2,1)S(1)} %collective-permute-done.other, bf16[2,512,512]{2,1,0:T(8,128)(2,1)S(1)} %copy-done.2, ...), custom_call_target="tpu_custom_call" | custom-call | tf_op jit(solution)/shard_map/probe_step/pallas_call | solution.py:201
  67.4 3.8 %all-to-all-start.2 = ((bf16[128,4,8,128]{3,2,1,0:T(8,128)(2,1)}), bf16[128,4,8,128]{3,2,1,0:T(8,128)(2,1)S(1)}, u32[]{:S(2)}, u32[]{:S(2)}) async-start(bf16[128,4,8,128]{3,2,1,0:T(8,128)(2,1)} %bitcast.29), calls=%async_computation.2 | async-start | bytes 2097152 | tf_op jit(solution)/shard_map/all_to_all | solution.py:369
  71.2 0.7 pad_add_fusion.meta
  71.9 1.3 %slice.59 = f32[1,1]{1,0:T(1,128)} slice(f32[8,128]{1,0:T(8,128)} %get-tuple-element.15), slice={[0:1], [0:1]} | slice | bytes 8 | tf_op jit(solution)/shard_map/slice | solution.py:377
  73.1 1.6 %collective-permute-start.1 = (f32[1]{0:T(128)}, f32[1]{0:T(128)}, u32[]{:S(2)}, u32[]{:S(2)}) collective-permute-start(f32[1]{0:T(128)} %bitcast.36), channel_id=1, source_target_pairs={{0,2},{2,0},{1,3},{3,1},{4,6},{6,4},{5,7},{7,5},{8,10},{10,8},{9,1... | collective-permute-start | bytes 20 | tf_op jit(solution)/shard_map/ppermute | solution.py:378
  74.8 5.3 %collective-permute-done.1 = f32[1]{0:T(128)} collective-permute-done((f32[1]{0:T(128)}, f32[1]{0:T(128)}, u32[]{:S(2)}, u32[]{:S(2)}) %collective-permute-start.1) | collective-permute-done | bytes 36 | tf_op jit(solution)/shard_map/ppermute | solution.py:378
  80.1 1.3 %pad_maximum_fusion = f32[2]{0:T(128)S(1)} fusion(f32[1]{0:T(128)} %collective-permute-done.1, f32[1]{0:T(128)} %bitcast.36), kind=kLoop, calls=%fused_computation.69 | loop fusion | flops 2 | bytes 16 | tf_op jit(solution)/shard_map/concatenate | solution.py:379
  81.4 0.1 rev.3
  81.5 9.1 %all-to-all-done.2 = bf16[128,4,8,128]{3,2,1,0:T(8,128)(2,1)S(1)} async-done(((bf16[128,4,8,128]{3,2,1,0:T(8,128)(2,1)}), bf16[128,4,8,128]{3,2,1,0:T(8,128)(2,1)S(1)}, u32[]{:S(2)}, u32[]{:S(2)}) %all-to-all-start.2) | async-done | bytes 1048608 | tf_op jit(solution)/shard_map/all_to_all | solution.py:369
  90.7 2.3 %sum_step.1 = bf16[8,4,8,256]{3,2,1,0:T(8,128)(2,1)} custom-call(s32[130]{0:T(256)} %pad_add_fusion.meta, bf16[64,2,4,8,128]{4,3,2,1,0:T(8,128)(2,1)S(1)} %bitcast.75), custom_call_target="tpu_custom_call" | custom-call | tf_op jit(solution)/shard_map/sum_step/pallas_call | solution.py:318
  93.0 3.7 %all-to-all-start.3 = ((bf16[8,4,8,256]{3,2,1,0:T(8,128)(2,1)}), bf16[8,4,8,256]{3,2,1,0:T(8,128)(2,1)S(1)}, u32[]{:S(2)}, u32[]{:S(2)}) async-start(bf16[8,4,8,256]{3,2,1,0:T(8,128)(2,1)} %sum_step.1), calls=%async_computation.3 | async-start | bytes 262144 | tf_op jit(solution)/shard_map/all_to_all | solution.py:372
  96.7 1.8 %broadcast_select_fusion = f32[2]{0:T(128)} fusion(f32[2]{0:T(128)S(1)} %rev.3, pred[]{:T(512)S(6)} %eq.121, f32[1]{0:T(128)} %collective-permute-done.1, f32[1]{0:T(128)} %bitcast.36), kind=kLoop, calls=%fused_computation.66 | loop fusion | flops 4 | bytes 25 | tf_op jit(solution)/shard_map/jit(_where)/select_n | solution.py:380
  98.5 4.0 %all-to-all-done.3 = bf16[8,4,8,256]{3,2,1,0:T(8,128)(2,1)S(1)} async-done(((bf16[8,4,8,256]{3,2,1,0:T(8,128)(2,1)}), bf16[8,4,8,256]{3,2,1,0:T(8,128)(2,1)S(1)}, u32[]{:S(2)}, u32[]{:S(2)}) %all-to-all-start.3) | async-done | bytes 131104 | tf_op jit(solution)/shard_map/all_to_all | solution.py:372
  102.5 1.1 %fusion.8 = f32[512,4,32]{0,2,1:T(8,128)} fusion(bf16[4,32,512]{2,1,0:T(8,128)(2,1)S(1)} %bitcast.81, s32[512]{0:T(512)S(1)} %fusion.20), kind=kOutput, calls=%fused_computation.18 | convolution fusion | flops 67371008 | bytes 395264 | tf_op jit(solution)/shard_map/dot_general | solution.py:374
  (12 shorter events, 0.2 us)
Async XLA Ops:
  0.6 0.9 copy-start.3
  3.5 22.9 %all-to-all-start = ((bf16[128,8,128]{2,1,0:T(8,128)(2,1)}), bf16[128,8,128]{2,1,0:T(8,128)(2,1)S(1)}, u32[]{:S(2)}, u32[]{:S(2)}) async-start(bf16[128,8,128]{2,1,0:T(8,128)(2,1)} %bitcast.3), calls=%async_computation | async-start | bytes 524288 | tf_op jit(solution)/shard_map/all_to_all | solution.py:340
  18.9 1.0 copy-start.1
  28.2 26.6 %copy-start = (bf16[1024,1024]{1,0:T(8,128)(2,1)S(1)}, bf16[1024,1024]{1,0:T(8,128)(2,1)}, u32[]{:S(2)}) copy-start(bf16[1024,1024]{1,0:T(8,128)(2,1)} %constant.146.bq) | copy-start | bytes 6291460
  28.2 26.6 %copy-start.2 = (bf16[2,512,512]{2,1,0:T(8,128)(2,1)S(1)}, bf16[2,512,512]{2,1,0:T(8,128)(2,1)}, u32[]{:S(2)}) copy-start(bf16[2,512,512]{2,1,0:T(8,128)(2,1)} %copy-done.1) | copy-start | bytes 3145732
  52.1 2.7 %collective-permute-start = (bf16[32,2,2,4,8,128]{5,4,3,2,1,0:T(8,128)(2,1)S(1)}, bf16[32,2,2,4,8,128]{5,4,3,2,1,0:T(8,128)(2,1)S(1)}, u32[]{:S(2)}, u32[]{:S(2)}) collective-permute-start(bf16[32,2,2,4,8,128]{5,4,3,2,1,0:T(8,128)(2,1)S(1)} %bitcast.73), channel_id=1, source_target_pairs={{0,1},{1,0},{2,3},{3,2},{4,5},{5,4},{6,7},{7,6},{8,9},{9,8},{10,11... | collective-permute-start | bytes 3145736 | tf_op jit(solution)/shard_map/ppermute | solution.py:365
  67.4 23.3 %all-to-all-start.2 = ((bf16[128,4,8,128]{3,2,1,0:T(8,128)(2,1)}), bf16[128,4,8,128]{3,2,1,0:T(8,128)(2,1)S(1)}, u32[]{:S(2)}, u32[]{:S(2)}) async-start(bf16[128,4,8,128]{3,2,1,0:T(8,128)(2,1)} %bitcast.29), calls=%async_computation.2 | async-start | bytes 2097152 | tf_op jit(solution)/shard_map/all_to_all | solution.py:369
  73.1 7.0 %collective-permute-start.1 = (f32[1]{0:T(128)}, f32[1]{0:T(128)}, u32[]{:S(2)}, u32[]{:S(2)}) collective-permute-start(f32[1]{0:T(128)} %bitcast.36), channel_id=1, source_target_pairs={{0,2},{2,0},{1,3},{3,1},{4,6},{6,4},{5,7},{7,5},{8,10},{10,8},{9,1... | collective-permute-start | bytes 20 | tf_op jit(solution)/shard_map/ppermute | solution.py:378
  93.0 9.5 %all-to-all-start.3 = ((bf16[8,4,8,256]{3,2,1,0:T(8,128)(2,1)}), bf16[8,4,8,256]{3,2,1,0:T(8,128)(2,1)S(1)}, u32[]{:S(2)}, u32[]{:S(2)}) async-start(bf16[8,4,8,256]{3,2,1,0:T(8,128)(2,1)} %sum_step.1), calls=%async_computation.3 | async-start | bytes 262144 | tf_op jit(solution)/shard_map/all_to_all | solution.py:372

commit v5 on v4

--- a/solution.py
+++ b/solution.py
@@ -306,7 +306,7 @@
                     acc[1, tile, plane, c] += jnp.where(right, piece, 0.0)
         return 0
 
-    lax.fori_loop(0, 64, step, 0, unroll=4)
+    lax.fori_loop(0, 64, step, 0, unroll=8)
     for h in range(2):
         for tile in range(4):
             for plane in range(4):

time: 104 us -> 104 us (level)
  no operation moved by 1% of the time
where the time goes in v5:
time: 104 us
  waiting for transfers between devices  27.2 us (26%)
  blocking collectives  23 us (22%)
  starting transfers between devices  21 us (20%)
  Pallas kernels  20.8 us (20%)
  other arithmetic  5.78 us (6%)
  local copies, waits for them, and re-layouts  3.87 us (4%)
  matrix products  1.05 us (1%)
    all_to_all x1, blocking collectives, body(): lax.all_to_all(sent.reshape(128, 4, 8, 128), ALL, 0, 0, tiled=True)  23 us
    pallas_call x1, Pallas kernels, probe_step(): pl.pallas_call(probe_kernel, out_shape=(pltpu.VMEM((2, 16, 2, 2, 4, 8, 12...  12.6 us
    all_to_all x1, starting transfers between devices, body(): got = lax.all_to_all(sent.reshape(128, 8, 128), ALL, 0, 0, tiled=True)  11.5 us
    all_to_all x1, waiting for transfers between devices, body(): home = lax.all_to_all(grad.reshape(128, 4, 8, 128), ALL, 0, 0, tiled=True)  9.13 us
    all_to_all x1, waiting for transfers between devices, body(): got = lax.all_to_all(sent.reshape(128, 8, 128), ALL, 0, 0, tiled=True)  6.42 us
    ppermute x1, waiting for transfers between devices, body(): loss_other = lax.ppermute(loss, 'zl', [(0, 1), (1, 0)])  5.34 us
    all_to_all x1, waiting for transfers between devices, body(): final = lax.all_to_all(sums, SHARERS, 0, 0, tiled=True)  4.01 us
    pallas_call x1, Pallas kernels, roll_step(): pl.pallas_call(roll_kernel, out_shape=(pltpu.VMEM((2, FRAME, FRAME), BF),...  3.95 us
  transfers between devices with their start and end apart: 5, of which 5 were waited for; matrix products, arithmetic and copies ran while one was open for 5% of the time, Pallas kernels for 4%

profile of v5, /device:TPU:1, one launch (start us, length us, event | category | flops | bytes accessed | tf_op | source)
XLA Modules:
  0.0 103.6 jit_solution(10018568973677233735)
XLA Ops:
  0.6 0.0 copy-start.3
  0.6 0.9 copy-done.3
  1.5 1.9 %prepare_step.1 = bf16[32,2,2,8,128]{4,3,2,1,0:T(8,128)(2,1)} custom-call(s32[2,2]{1,0:T(2,128)} %positions.3, s32[2]{0:T(128)} %owner.3, bf16[128,512]{1,0:T(8,128)(2,1)S(1)} %bitcast.76), custom_call_target="tpu_custom_call" | custom-call | tf_op jit(solution)/shard_map/prepare_step/pallas_call | solution.py:248
  3.5 11.5 %all-to-all-start = ((bf16[128,8,128]{2,1,0:T(8,128)(2,1)}), bf16[128,8,128]{2,1,0:T(8,128)(2,1)S(1)}, u32[]{:S(2)}, u32[]{:S(2)}) async-start(bf16[128,8,128]{2,1,0:T(8,128)(2,1)} %bitcast.3), calls=%async_computation | async-start | bytes 524288 | tf_op jit(solution)/shard_map/all_to_all | solution.py:340
  15.0 4.0 %roll_step.1 = (bf16[2,512,512]{2,1,0:T(8,128)(2,1)S(1)}, f32[512,512]{1,0:T(8,128)}) custom-call(s32[2,2]{1,0:T(2,128)} %positions.3, s32[2]{0:T(128)} %owner.3, s32[1]{0:T(128)} %bitcast.4.which, bf16[2,512,512]{2,1,0:T(8,128)(2,1)} %illumination.1, f32[2,512,512]{2,1,0:T(8,128)} %intensities.1), custom_call_target="tpu_custom_call" | custom-call | tf_op jit(solution)/shard_map/roll_step/pallas_call | solution.py:275
  18.9 0.0 copy-start.1
  18.9 1.0 copy-done.1
  19.9 6.4 %all-to-all-done = bf16[128,8,128]{2,1,0:T(8,128)(2,1)S(1)} async-done(((bf16[128,8,128]{2,1,0:T(8,128)(2,1)}), bf16[128,8,128]{2,1,0:T(8,128)(2,1)S(1)}, u32[]{:S(2)}, u32[]{:S(2)}) %all-to-all-start) | async-done | bytes 262176 | tf_op jit(solution)/shard_map/all_to_all | solution.py:340
  26.4 0.1 convert_reduce_fusion
  26.5 0.1 reshape.253
  26.5 0.2 fusion.12
  26.8 0.1 lt.70
  26.9 0.1 lt.71
  27.0 0.2 fusion.28
  27.3 0.1 compare_select_fusion
  27.3 0.1 convert_add_fusion
  27.5 0.7 add_compare_fusion.7
  28.2 0.0 copy-start
  28.2 0.0 copy-start.2
  28.2 0.8 fusion.6
  29.1 23.0 %all_to_all.20 = bf16[128,4,8,128]{3,2,1,0:T(8,128)(2,1)S(1)} all-to-all(bf16[128,4,8,128]{3,2,1,0:T(8,128)(2,1)S(1)} %fusion.6), channel_id=1, replica_groups=mesh['half'=2,'col'=16,'zl'=2,'core'=2] {'half','col','zl','core'}, dimensions={0} | all-to-all | bytes 2097152 | tf_op jit(solution)/shard_map/all_to_all | solution.py:364
  52.1 0.4 collective-permute-start
  52.5 2.3 %collective-permute-done.other = bf16[32,2,2,4,8,128]{5,4,3,2,1,0:T(8,128)(2,1)S(1)} collective-permute-done((bf16[32,2,2,4,8,128]{5,4,3,2,1,0:T(8,128)(2,1)S(1)}, bf16[32,2,2,4,8,128]{5,4,3,2,1,0:T(8,128)(2,1)S(1)}, u32[]{:S(2)}, u32[]{:S(2)}) %collective-permute-start) | collective-permute-done | bytes 1048608 | tf_op jit(solution)/shard_map/ppermute | solution.py:365
  54.8 0.0 copy-done
  54.8 0.0 copy-done.2
  54.8 12.6 %probe_step.1 = (bf16[2,16,2,2,4,8,128]{6,5,4,3,2,1,0:T(8,128)(2,1)}, f32[8,128]{1,0:T(8,128)}) custom-call(s32[1]{0:T(128)} %bitcast.5.core_ref, bf16[32,2,2,4,8,128]{5,4,3,2,1,0:T(8,128)(2,1)S(1)} %bitcast.74, bf16[32,2,2,4,8,128]{5,4,3,2,1,0:T(8,128)(2,1)S(1)} %collective-permute-done.other, bf16[2,512,512]{2,1,0:T(8,128)(2,1)S(1)} %copy-done.2, ...), custom_call_target="tpu_custom_call" | custom-call | tf_op jit(solution)/shard_map/probe_step/pallas_call | solution.py:201
  67.4 3.8 %all-to-all-start.2 = ((bf16[128,4,8,128]{3,2,1,0:T(8,128)(2,1)}), bf16[128,4,8,128]{3,2,1,0:T(8,128)(2,1)S(1)}, u32[]{:S(2)}, u32[]{:S(2)}) async-start(bf16[128,4,8,128]{3,2,1,0:T(8,128)(2,1)} %bitcast.29), calls=%async_computation.2 | async-start | bytes 2097152 | tf_op jit(solution)/shard_map/all_to_all | solution.py:369
  71.2 0.7 pad_add_fusion.meta
  71.9 1.3 %slice.59 = f32[1,1]{1,0:T(1,128)} slice(f32[8,128]{1,0:T(8,128)} %get-tuple-element.15), slice={[0:1], [0:1]} | slice | bytes 8 | tf_op jit(solution)/shard_map/slice | solution.py:377
  73.1 1.6 %collective-permute-start.1 = (f32[1]{0:T(128)}, f32[1]{0:T(128)}, u32[]{:S(2)}, u32[]{:S(2)}) collective-permute-start(f32[1]{0:T(128)} %bitcast.36), channel_id=1, source_target_pairs={{0,2},{2,0},{1,3},{3,1},{4,6},{6,4},{5,7},{7,5},{8,10},{10,8},{9,1... | collective-permute-start | bytes 20 | tf_op jit(solution)/shard_map/ppermute | solution.py:378
  74.8 5.3 %collective-permute-done.1 = f32[1]{0:T(128)} collective-permute-done((f32[1]{0:T(128)}, f32[1]{0:T(128)}, u32[]{:S(2)}, u32[]{:S(2)}) %collective-permute-start.1) | collective-permute-done | bytes 36 | tf_op jit(solution)/shard_map/ppermute | solution.py:378
  80.1 1.3 %pad_maximum_fusion = f32[2]{0:T(128)S(1)} fusion(f32[1]{0:T(128)} %collective-permute-done.1, f32[1]{0:T(128)} %bitcast.36), kind=kLoop, calls=%fused_computation.69 | loop fusion | flops 2 | bytes 16 | tf_op jit(solution)/shard_map/concatenate | solution.py:379
  81.4 0.1 rev.3
  81.5 9.1 %all-to-all-done.2 = bf16[128,4,8,128]{3,2,1,0:T(8,128)(2,1)S(1)} async-done(((bf16[128,4,8,128]{3,2,1,0:T(8,128)(2,1)}), bf16[128,4,8,128]{3,2,1,0:T(8,128)(2,1)S(1)}, u32[]{:S(2)}, u32[]{:S(2)}) %all-to-all-start.2) | async-done | bytes 1048608 | tf_op jit(solution)/shard_map/all_to_all | solution.py:369
  90.7 2.3 %sum_step.1 = bf16[8,4,8,256]{3,2,1,0:T(8,128)(2,1)} custom-call(s32[130]{0:T(256)} %pad_add_fusion.meta, bf16[64,2,4,8,128]{4,3,2,1,0:T(8,128)(2,1)S(1)} %bitcast.75), custom_call_target="tpu_custom_call" | custom-call | tf_op jit(solution)/shard_map/sum_step/pallas_call | solution.py:318
  93.0 3.7 %all-to-all-start.3 = ((bf16[8,4,8,256]{3,2,1,0:T(8,128)(2,1)}), bf16[8,4,8,256]{3,2,1,0:T(8,128)(2,1)S(1)}, u32[]{:S(2)}, u32[]{:S(2)}) async-start(bf16[8,4,8,256]{3,2,1,0:T(8,128)(2,1)} %sum_step.1), calls=%async_computation.3 | async-start | bytes 262144 | tf_op jit(solution)/shard_map/all_to_all | solution.py:372
  96.7 1.8 %broadcast_select_fusion = f32[2]{0:T(128)} fusion(f32[2]{0:T(128)S(1)} %rev.3, pred[]{:T(512)S(6)} %eq.121, f32[1]{0:T(128)} %collective-permute-done.1, f32[1]{0:T(128)} %bitcast.36), kind=kLoop, calls=%fused_computation.66 | loop fusion | flops 4 | bytes 25 | tf_op jit(solution)/shard_map/jit(_where)/select_n | solution.py:380
  98.5 4.0 %all-to-all-done.3 = bf16[8,4,8,256]{3,2,1,0:T(8,128)(2,1)S(1)} async-done(((bf16[8,4,8,256]{3,2,1,0:T(8,128)(2,1)}), bf16[8,4,8,256]{3,2,1,0:T(8,128)(2,1)S(1)}, u32[]{:S(2)}, u32[]{:S(2)}) %all-to-all-start.3) | async-done | bytes 131104 | tf_op jit(solution)/shard_map/all_to_all | solution.py:372
  102.5 1.1 %fusion.8 = f32[512,4,32]{0,2,1:T(8,128)} fusion(bf16[4,32,512]{2,1,0:T(8,128)(2,1)S(1)} %bitcast.81, s32[512]{0:T(512)S(1)} %fusion.20), kind=kOutput, calls=%fused_computation.18 | convolution fusion | flops 67371008 | bytes 395264 | tf_op jit(solution)/shard_map/dot_general | solution.py:374
  (12 shorter events, 0.2 us)
Async XLA Ops:
  0.6 0.9 copy-start.3
  3.5 22.9 %all-to-all-start = ((bf16[128,8,128]{2,1,0:T(8,128)(2,1)}), bf16[128,8,128]{2,1,0:T(8,128)(2,1)S(1)}, u32[]{:S(2)}, u32[]{:S(2)}) async-start(bf16[128,8,128]{2,1,0:T(8,128)(2,1)} %bitcast.3), calls=%async_computation | async-start | bytes 524288 | tf_op jit(solution)/shard_map/all_to_all | solution.py:340
  18.9 1.0 copy-start.1
  28.2 26.6 %copy-start = (bf16[1024,1024]{1,0:T(8,128)(2,1)S(1)}, bf16[1024,1024]{1,0:T(8,128)(2,1)}, u32[]{:S(2)}) copy-start(bf16[1024,1024]{1,0:T(8,128)(2,1)} %constant.146.bq) | copy-start | bytes 6291460
  28.2 26.6 %copy-start.2 = (bf16[2,512,512]{2,1,0:T(8,128)(2,1)S(1)}, bf16[2,512,512]{2,1,0:T(8,128)(2,1)}, u32[]{:S(2)}) copy-start(bf16[2,512,512]{2,1,0:T(8,128)(2,1)} %copy-done.1) | copy-start | bytes 3145732
  52.1 2.7 %collective-permute-start = (bf16[32,2,2,4,8,128]{5,4,3,2,1,0:T(8,128)(2,1)S(1)}, bf16[32,2,2,4,8,128]{5,4,3,2,1,0:T(8,128)(2,1)S(1)}, u32[]{:S(2)}, u32[]{:S(2)}) collective-permute-start(bf16[32,2,2,4,8,128]{5,4,3,2,1,0:T(8,128)(2,1)S(1)} %bitcast.73), channel_id=1, source_target_pairs={{0,1},{1,0},{2,3},{3,2},{4,5},{5,4},{6,7},{7,6},{8,9},{9,8},{10,11... | collective-permute-start | bytes 3145736 | tf_op jit(solution)/shard_map/ppermute | solution.py:365
  67.4 23.3 %all-to-all-start.2 = ((bf16[128,4,8,128]{3,2,1,0:T(8,128)(2,1)}), bf16[128,4,8,128]{3,2,1,0:T(8,128)(2,1)S(1)}, u32[]{:S(2)}, u32[]{:S(2)}) async-start(bf16[128,4,8,128]{3,2,1,0:T(8,128)(2,1)} %bitcast.29), calls=%async_computation.2 | async-start | bytes 2097152 | tf_op jit(solution)/shard_map/all_to_all | solution.py:369
  73.1 7.0 %collective-permute-start.1 = (f32[1]{0:T(128)}, f32[1]{0:T(128)}, u32[]{:S(2)}, u32[]{:S(2)}) collective-permute-start(f32[1]{0:T(128)} %bitcast.36), channel_id=1, source_target_pairs={{0,2},{2,0},{1,3},{3,1},{4,6},{6,4},{5,7},{7,5},{8,10},{10,8},{9,1... | collective-permute-start | bytes 20 | tf_op jit(solution)/shard_map/ppermute | solution.py:378
  93.0 9.5 %all-to-all-start.3 = ((bf16[8,4,8,256]{3,2,1,0:T(8,128)(2,1)}), bf16[8,4,8,256]{3,2,1,0:T(8,128)(2,1)S(1)}, u32[]{:S(2)}, u32[]{:S(2)}) async-start(bf16[8,4,8,256]{3,2,1,0:T(8,128)(2,1)} %sum_step.1), calls=%async_computation.3 | async-start | bytes 262144 | tf_op jit(solution)/shard_map/all_to_all | solution.py:372
